TPU v7x, 16 devices: a whole 2x2x2 slice. The times are simulated.
16 devices in a mesh: sp: 16 (over z, y, x, core).
Axes of the slice: x: 2, y: 2, z: 2, core: 2. Of those that a mesh axis runs over, the one named last changes fastest.
Arguments:
- hidden: bfloat16 [64, 512, 2048], P(None, 'sp')
- norm_gain: bfloat16 [2048], replicated
- w_qkv: bfloat16 [2048, 6144], replicated
- w_out: bfloat16 [2048, 2048], replicated
- cos_tab: float32 [512, 64], P('sp')
- sin_tab: float32 [512, 64], P('sp')
- d_out: bfloat16 [64, 512, 2048], P(None, 'sp')
Outputs:
- output 1: bfloat16 [64, 512, 2048], P(None, 'sp')
- output 2: bfloat16 [64, 512, 2048], P(None, 'sp')
- output 3: float32 [2048, 6144], replicated
- output 4: float32 [2048, 2048], replicated
- output 5: float32 [2048], replicated
All inputs are finite; a program needn't handle non-finite values.
Results may differ from a plain program's by a relative error of at most 0.011258.
Values are sent between devices in bfloat16 or wider.
A program may use at most 1 GiB of HBM per device.

v0:
```python
import functools
import jax
import jax.numpy as jnp
from jax import lax
from jax.sharding import PartitionSpec as P

NORM_EPS = 1e-6


def rotate_half(head_vecs):
    half_dim = head_vecs.shape[-1] // 2
    return jnp.concatenate([-head_vecs[..., half_dim:], head_vecs[..., :half_dim]], axis=-1)


def rotate_half_transpose(head_vecs):
    half_dim = head_vecs.shape[-1] // 2
    return jnp.concatenate([head_vecs[..., half_dim:], -head_vecs[..., :half_dim]], axis=-1)


def solution(mesh):
    group_size = mesh.shape['sp']
    token_spec = P(None, 'sp', None)
    table_spec = P('sp', None)
    to_heads = functools.partial(lax.all_to_all, axis_name='sp', split_axis=2, concat_axis=1, tiled=True)
    to_tokens = functools.partial(lax.all_to_all, axis_name='sp', split_axis=1, concat_axis=2, tiled=True)

    def device_step(hidden, norm_gain, w_qkv, w_out, cos_tab, sin_tab, d_out):
        num_seqs, local_len, model_dim = hidden.shape
        head_dim = 2 * cos_tab.shape[1]
        num_heads = model_dim // head_dim
        full_len = local_len * group_size
        score_scale = head_dim ** -0.5
        hidden_f32 = hidden.astype(jnp.float32)
        gain_f32 = norm_gain.astype(jnp.float32)
        inv_rms = lax.rsqrt(jnp.mean(hidden_f32 * hidden_f32, axis=-1, keepdims=True) + NORM_EPS)
        normed = (hidden_f32 * inv_rms * gain_f32).astype(jnp.bfloat16)
        projected = jnp.einsum('btd,de->bte', normed, w_qkv, preferred_element_type=jnp.float32)
        projected = projected.reshape(num_seqs, local_len, 3, num_heads, head_dim)
        cos_full = jnp.concatenate([cos_tab, cos_tab], axis=-1)[:, None, :]
        sin_full = jnp.concatenate([sin_tab, sin_tab], axis=-1)[:, None, :]
        q_local = (projected[:, :, 0] * cos_full + rotate_half(projected[:, :, 0]) * sin_full).astype(jnp.bfloat16)
        k_local = (projected[:, :, 1] * cos_full + rotate_half(projected[:, :, 1]) * sin_full).astype(jnp.bfloat16)
        v_local = projected[:, :, 2].astype(jnp.bfloat16)
        q_heads = to_heads(q_local)
        k_heads = to_heads(k_local)
        v_heads = to_heads(v_local)
        row_pos = lax.broadcasted_iota(jnp.int32, (full_len, full_len), 0)
        col_pos = lax.broadcasted_iota(jnp.int32, (full_len, full_len), 1)
        scores = jnp.einsum('bqhd,bkhd->bhqk', q_heads, k_heads, preferred_element_type=jnp.float32) * score_scale
        probs_f32 = jax.nn.softmax(jnp.where(row_pos >= col_pos, scores, -1e30), axis=-1)
        probs_bf = probs_f32.astype(jnp.bfloat16)
        attn_heads = jnp.einsum('bhqk,bkhd->bqhd', probs_bf, v_heads, preferred_element_type=jnp.float32).astype(jnp.bfloat16)
        attn_local = to_tokens(attn_heads).reshape(num_seqs, local_len, model_dim)
        out_proj = jnp.einsum('btd,de->bte', attn_local, w_out, preferred_element_type=jnp.float32)
        y_out = (hidden_f32 + out_proj).astype(jnp.bfloat16)
        dw_out = lax.psum(jnp.einsum('btd,bte->de', attn_local, d_out, preferred_element_type=jnp.float32), 'sp')
        d_attn = jnp.einsum('bte,de->btd', d_out, w_out, preferred_element_type=jnp.float32).astype(jnp.bfloat16)
        d_attn_heads = to_heads(d_attn.reshape(num_seqs, local_len, num_heads, head_dim))
        d_values = jnp.einsum('bhqk,bqhd->bkhd', probs_bf, d_attn_heads, preferred_element_type=jnp.float32).astype(jnp.bfloat16)
        d_probs = jnp.einsum('bqhd,bkhd->bhqk', d_attn_heads, v_heads, preferred_element_type=jnp.float32)
        d_scores = (probs_f32 * (d_probs - jnp.sum(probs_f32 * d_probs, axis=-1, keepdims=True)) * score_scale).astype(jnp.bfloat16)
        d_queries = jnp.einsum('bhqk,bkhd->bqhd', d_scores, k_heads, preferred_element_type=jnp.float32).astype(jnp.bfloat16)
        d_keys = jnp.einsum('bhqk,bqhd->bkhd', d_scores, q_heads, preferred_element_type=jnp.float32).astype(jnp.bfloat16)
        dq_f32 = to_tokens(d_queries).astype(jnp.float32)
        dk_f32 = to_tokens(d_keys).astype(jnp.float32)
        dv_local = to_tokens(d_values)
        dq_in = dq_f32 * cos_full + rotate_half_transpose(dq_f32 * sin_full)
        dk_in = dk_f32 * cos_full + rotate_half_transpose(dk_f32 * sin_full)
        d_proj = jnp.stack([dq_in.astype(jnp.bfloat16), dk_in.astype(jnp.bfloat16), dv_local], axis=2).reshape(num_seqs, local_len, 3 * model_dim)
        dw_qkv = lax.psum(jnp.einsum('btd,bte->de', normed, d_proj, preferred_element_type=jnp.float32), 'sp')
        d_normed = jnp.einsum('bte,de->btd', d_proj, w_qkv, preferred_element_type=jnp.float32).astype(jnp.bfloat16).astype(jnp.float32)
        d_gain = lax.psum(jnp.sum(d_normed * hidden_f32 * inv_rms, axis=(0, 1)), 'sp')
        d_scaled = d_normed * gain_f32
        d_hidden = d_out.astype(jnp.float32) + inv_rms * d_scaled - hidden_f32 * inv_rms ** 3 * jnp.mean(d_scaled * hidden_f32, axis=-1, keepdims=True)
        return y_out, d_hidden.astype(jnp.bfloat16), dw_qkv, dw_out, d_gain

    return jax.shard_map(device_step, mesh=mesh, in_specs=(token_spec, P(None), P(None, None), P(None, None), table_spec, table_spec, token_spec), out_specs=(token_spec, token_spec, P(None, None), P(None, None), P(None)), check_vma=False)
```

profile of v0, /device:TPU:0, one launch (start us, length us, event | category | flops | bytes accessed | tf_op | source)
XLA Modules:
  0.0 2153.6 jit_solution(10651755457614059951)
XLA Ops:
  13.6 61.9 %fusion.17 = f32[64,32,6144]{2,1,0:T(8,128)} fusion(bf16[2048,6144]{1,0:T(8,128)(2,1)} %param.9, bf16[64,32,2048]{2,1,0:T(8,128)(2,1)} %param.7, f32[2048]{0:T(1024)S(1)} %convert_element_type.154, f32[64,32]{1,0:T(8,128)S(1)} %get-tuple-element.20), kind=kOutput, calls=%fused_computation.24 | convolution fusion | flops 51556384768 | bytes 83902464 | tf_op jit(solution)/shard_map/btd,de->bte/dot_general | solution.py:37
  75.4 41.2 %copy.96 = f32[256,8,48,128]{3,2,1,0:T(8,128)} copy(f32[256,8,48,128]{3,1,2,0:T(8,128)} %bitcast.156) | data formatting | bytes 100663296
  116.6 21.9 %fusion.79 = (f32[64,32,1,16,128]{4,3,2,1,0:T(8,128)}, f32[64,32,1,16,128]{4,3,2,1,0:T(8,128)}) fusion(f32[64,32,3,16,128]{4,3,2,1,0:T(8,128)} %bitcast.150), kind=kLoop, calls=%fused_computation.98 | loop fusion | bytes 67108864 | tf_op jit(solution)/shard_map/slice | solution.py:42
  138.6 23.9 %copy_bitcast_fusion = (f32[64,32,16,128]{3,1,2,0:T(8,128)}, f32[64,32,16,128]{3,1,2,0:T(8,128)S(1)}) fusion(f32[64,32,1,16,128]{4,3,2,1,0:T(8,128)} %get-tuple-element.9, f32[64,32,1,16,128]{4,3,2,1,0:T(8,128)} %get-tuple-element.10), kind=kLoop, calls=%fused_computation.66 | loop fusion | bytes 67108864 | tf_op jit(solution)/shard_map/squeeze | solution.py:42
  162.4 23.9 %slice_negate_fusion.2 = (f32[64,32,16,64]{3,1,2,0:T(8,128)}, f32[64,32,16,64]{3,1,2,0:T(8,128)}) fusion(f32[64,32,16,128]{3,1,2,0:T(8,128)} %get-tuple-element.30), kind=kLoop, calls=%fused_computation.58 | loop fusion | flops 2097152 | bytes 33554432 | tf_op jit(solution)/shard_map/neg | solution.py:12
  198.8 42.1 %fusion.44 = (bf16[64,32,16,128]{3,1,2,0:T(8,128)(2,1)}, bf16[64,32,16,128]{3,1,2,0:T(8,128)(2,1)}) fusion(f32[64,32,16,64]{3,1,2,0:T(8,128)} %get-tuple-element.16, f32[64,32,16,64]{3,1,2,0:T(8,128)} %get-tuple-element.15, f32[32,128]{1,0:T(8,128)S(1)} %get-tuple-element.33, f32[32,128]{1,0:T(8,128)S(1)} %get-tuple-element.32, ...), kind=kLoop, calls=%fused_computation.65 | loop fusion | flops 41943040 | bytes 83918848 | tf_op jit(solution)/shard_map/convert_element_type | solution.py:42
  264.2 97.9 %all-to-all-done.2 = bf16[64,32,16,128]{3,1,0,2:T(8,128)(2,1)} async-done(((bf16[64,32,16,128]{3,1,0,2:T(8,128)(2,1)}), bf16[64,32,16,128]{3,1,0,2:T(8,128)(2,1)}, u32[]{:S(2)}, u32[]{:S(2)}) %all-to-all-start.2) | async-done | bytes 8388640 | tf_op jit(solution)/shard_map/all_to_all | solution.py:45
  366.4 23.7 %convert_bitcast_fusion.7 = bf16[64,4,16,8,128]{4,3,2,1,0:T(8,128)(2,1)} fusion(bf16[64,32,2048]{2,1,0:T(8,128)(2,1)} %param.13, bf16[2048,2048]{1,0:T(8,128)(2,1)} %param.10), kind=kOutput, calls=%fused_computation.82 | convolution fusion | flops 17184063488 | bytes 25165824 | tf_op jit(solution)/shard_map/bte,de->btd/dot_general | solution.py:57
  399.0 74.3 %all-to-all-done.1 = bf16[64,32,16,128]{3,1,0,2:T(8,128)(2,1)} async-done(((bf16[64,32,16,128]{3,1,0,2:T(8,128)(2,1)}), bf16[64,32,16,128]{3,1,0,2:T(8,128)(2,1)}, u32[]{:S(2)}, u32[]{:S(2)}) %all-to-all-start.1) | async-done | bytes 8388640 | tf_op jit(solution)/shard_map/all_to_all | solution.py:44
  495.4 88.8 %all-to-all-done.4 = bf16[64,32,16,128]{3,1,0,2:T(8,128)(2,1)} async-done(((bf16[64,32,16,128]{3,1,0,2:T(8,128)(2,1)}), bf16[64,32,16,128]{3,1,0,2:T(8,128)(2,1)}, u32[]{:S(2)}, u32[]{:S(2)}) %all-to-all-start.4) | async-done | bytes 8388640 | tf_op jit(solution)/shard_map/all_to_all | solution.py:58
  616.8 78.8 %all-to-all-done = bf16[64,32,16,128]{3,1,0,2:T(8,128)(2,1)} async-done(((bf16[64,32,16,128]{3,1,0,2:T(8,128)(2,1)}), bf16[64,32,16,128]{3,1,0,2:T(8,128)(2,1)}, u32[]{:S(2)}, u32[]{:S(2)}) %all-to-all-start) | async-done | bytes 8388640 | tf_op jit(solution)/shard_map/all_to_all | solution.py:46
  705.0 28.9 %fusion.81 = f32[64,512,512]{1,2,0:T(8,128)} fusion(bf16[64,512,128]{2,1,0:T(8,128)(2,1)} %bitcast.159, bf16[64,512,128]{2,1,0:T(8,128)(2,1)} %bitcast.157), kind=kOutput, calls=%fused_computation.100 | convolution fusion | flops 4294967296 | bytes 83886080 | tf_op jit(solution)/shard_map/bqhd,bkhd->bhqk/dot_general | solution.py:60
  733.9 33.6 %fusion.80 = (f32[64,512]{1,0:T(8,128)S(1)}, f32[64,512,512]{1,2,0:T(8,128)}) fusion(pred[512,512]{0,1:T(8,128)(4,1)S(1)} %iota_compare_fusion, bf16[64,512,128]{2,1,0:T(8,128)(2,1)} %bitcast.167, bf16[64,512,128]{2,1,0:T(8,128)(2,1)} %bitcast.165), kind=kOutput, calls=%fused_computation.99 | convolution fusion | flops 4362076672 | bytes 84279296 | tf_op jit(solution)/shard_map/sub | solution.py:50
  767.5 85.9 %convert_bitcast_fusion.5 = bf16[64,512,1,128]{1,3,0,2:T(8,128)(2,1)} fusion(bf16[64,512,128]{2,1,0:T(8,128)(2,1)} %bitcast.168, f32[64,512,512]{1,2,0:T(8,128)} %fusion.81, f32[64,512,512]{1,2,0:T(8,128)} %get-tuple-element.28, f32[64,512]{1,0:T(8,128)S(1)} %get-tuple-element.27), kind=kOutput, calls=%fused_computation.80 | convolution fusion | flops 4416635392 | bytes 151126016 | tf_op jit(solution)/shard_map/bhqk,bqhd->bkhd/dot_general | solution.py:63
  853.3 85.7 %convert_bitcast_fusion.6 = bf16[64,512,1,128]{1,3,0,2:T(8,128)(2,1)} fusion(bf16[64,512,128]{2,1,0:T(8,128)(2,1)} %bitcast.166, f32[64,512,512]{1,2,0:T(8,128)} %fusion.81, f32[64,512,512]{1,2,0:T(8,128)} %get-tuple-element.28, f32[64,512]{1,0:T(8,128)S(1)} %get-tuple-element.27), kind=kOutput, calls=%fused_computation.81 | convolution fusion | flops 4416635392 | bytes 151126016 | tf_op jit(solution)/shard_map/bhqk,bkhd->bqhd/dot_general | solution.py:62
  967.1 28.7 %convert_bitcast_fusion.4 = bf16[64,512,1,128]{1,3,0,2:T(8,128)(2,1)} fusion(bf16[64,512,128]{2,1,0:T(8,128)(2,1)} %bitcast.160, f32[64,512,512]{1,2,0:T(8,128)} %get-tuple-element.28, f32[64,512]{1,0:T(8,128)S(1)} %get-tuple-element.27), kind=kOutput, calls=%fused_computation.79 | convolution fusion | flops 4332716032 | bytes 84017152 | tf_op jit(solution)/shard_map/bhqk,bqhd->bkhd/dot_general | solution.py:59
  1007.9 54.2 %all-to-all-done.6 = bf16[64,512,1,128]{3,0,2,1:T(8,128)(2,1)} async-done(((bf16[64,512,1,128]{3,0,2,1:T(8,128)(2,1)}), bf16[64,512,1,128]{3,0,2,1:T(8,128)(2,1)}, u32[]{:S(2)}, u32[]{:S(2)}) %all-to-all-start.6) | async-done | bytes 8388640 | tf_op jit(solution)/shard_map/all_to_all | solution.py:65
  1066.1 27.9 %convert_bitcast_fusion.8 = bf16[64,512,1,128]{1,3,0,2:T(8,128)(2,1)} fusion(bf16[64,512,128]{2,1,0:T(8,128)(2,1)} %bitcast.158, f32[64,512,512]{1,2,0:T(8,128)} %get-tuple-element.28, f32[64,512]{1,0:T(8,128)S(1)} %get-tuple-element.27), kind=kOutput, calls=%fused_computation.83 | convolution fusion | flops 4332716032 | bytes 84017152 | tf_op jit(solution)/shard_map/bhqk,bkhd->bqhd/dot_general | solution.py:52
  1117.9 55.1 %all-to-all-done.5 = bf16[64,512,1,128]{3,0,2,1:T(8,128)(2,1)} async-done(((bf16[64,512,1,128]{3,0,2,1:T(8,128)(2,1)}), bf16[64,512,1,128]{3,0,2,1:T(8,128)(2,1)}, u32[]{:S(2)}, u32[]{:S(2)}) %all-to-all-start.5) | async-done | bytes 8388640 | tf_op jit(solution)/shard_map/all_to_all | solution.py:64
  1202.4 24.1 %slice_bitcast_fusion.1 = (f32[64,32,1,16,64]{4,1,3,0,2:T(8,128)}, f32[64,32,1,16,64]{4,1,3,0,2:T(8,128)}) fusion(f32[64,32,16,128]{3,1,2,0:T(8,128)} %get-tuple-element.25), kind=kLoop, calls=%fused_computation.57 | loop fusion | flops 2097152 | bytes 33554432 | tf_op jit(solution)/shard_map/concatenate | solution.py:17
  1239.0 34.8 %fusion.26 = (bf16[64,32,1,16,128]{4,1,3,0,2:T(8,128)(2,1)}, bf16[64,32,1,16,128]{4,1,3,0,2:T(8,128)(2,1)}) fusion(bf16[64,16,32,1,128]{4,2,1,0,3:T(8,128)(2,1)} %bitcast.155, f32[64,32,1,16,64]{4,1,3,0,2:T(8,128)} %get-tuple-element.12, f32[64,32,1,16,64]{4,1,3,0,2:T(8,128)} %get-tuple-element.11, f32[32,128]{1,0:T(8,128)S(1)} %copy-done.5, ...), kind=kLoop, calls=%fused_computation.38 | loop fusion | flops 41943040 | bytes 67125248 | tf_op jit(solution)/shard_map/convert_element_type | solution.py:69
  1300.6 17.8 pad_maximum_fusion
  1318.4 25.7 %copy.83 = bf16[64,32,3,16,128]{4,3,2,1,0:T(8,128)(2,1)} copy(bf16[64,32,3,16,128]{4,1,3,0,2:T(8,128)(2,1)} %pad_maximum_fusion) | data formatting | bytes 50331648 | tf_op jit(solution)/shard_map/stack | solution.py:69
  1344.1 35.5 %reshape.227 = bf16[64,32,6144]{2,1,0:T(8,128)(2,1)} reshape(bf16[64,32,3,16,128]{4,3,2,1,0:T(8,128)(2,1)} %copy.83) | data formatting | bytes 50331648 | tf_op jit(solution)/shard_map/reshape | solution.py:69
  1379.7 65.7 %convolution_bitcast_fusion = f32[2048,6144]{1,0:T(8,128)} fusion(bf16[64,32,6144]{2,1,0:T(8,128)(2,1)} %reshape.227, bf16[64,32,2048]{2,1,0:T(8,128)(2,1)} %param.7, f32[2048]{0:T(1024)S(1)} %copy-done.10, f32[64,32]{1,0:T(8,128)S(1)} %copy-done.8), kind=kOutput, calls=%fused_computation.20 | convolution fusion | flops 51556384768 | bytes 83902464 | tf_op jit(solution)/shard_map/btd,bte->de/dot_general | solution.py:70
  1457.5 15.3 copy.68
  1486.2 24.4 %convolution_bitcast_fusion.1 = f32[2048,2048]{1,0:T(8,128)} fusion(bf16[64,32,2048]{2,1,0:T(8,128)(2,1)} %reshape.224, bf16[64,32,2048]{2,1,0:T(8,128)(2,1)} %param.13), kind=kOutput, calls=%fused_computation.72 | convolution fusion | flops 17179869184 | bytes 33554432 | tf_op jit(solution)/shard_map/btd,bte->de/dot_general | solution.py:56
  1510.5 71.7 %fusion.38 = (f32[2048]{0:T(1024)S(1)}, f32[64,32]{1,0:T(8,128)S(1)}, bf16[64,32,2048]{2,1,0:T(8,128)(2,1)}) fusion(bf16[64,32,2048]{2,1,0:T(8,128)(2,1)} %param.7, f32[64,32]{1,0:T(8,128)S(1)} %copy-done.8, f32[2048]{0:T(1024)S(1)} %copy-done.10, bf16[64,32,6144]{2,1,0:T(8,128)(2,1)} %reshape.227, bf16[2048,6144]{1,0:T(8,128)(2,1)} %param.9), kind=kOutput, calls=%fused_computation.50 | convolution fusion | flops 51577356288 | bytes 67141632 | tf_op jit(solution)/shard_map/bte,de->btd/dot_general | solution.py:71
  1582.2 34.1 %psum.23 = f32[2048]{0:T(1024)} all-reduce(f32[2048]{0:T(1024)S(1)} %get-tuple-element.5), channel_id=1, replica_groups=mesh['sp'=16] {'sp'}, use_global_device_ids=true, to_apply=%region_8.9 | all-reduce | flops 2048 | bytes 16384 | tf_op jit(solution)/shard_map/psum | solution.py:72
  1632.5 22.3 %fusion.34 = bf16[64,32,2048]{2,1,0:T(8,128)(2,1)} fusion(bf16[64,32,2048]{2,1,0:T(8,128)(2,1)S(1)} %copy-done, bf16[64,32,2048]{2,1,0:T(8,128)(2,1)S(1)} %copy-done.1, bf16[2048,2048]{1,0:T(8,128)(2,1)} %param.10), kind=kOutput, calls=%fused_computation.46 | convolution fusion | flops 17192452096 | bytes 33554432 | tf_op jit(solution)/shard_map/btd,de->bte/dot_general | solution.py:54
  1654.8 445.4 %all-reduce.3.cloned.1.call-done = (f32[2048,6144]{1,0:T(8,128)}, f32[2048,2048]{1,0:T(8,128)}) async-done(((f32[2048,6144]{1,0:T(8,128)}, f32[2048,2048]{1,0:T(8,128)}), (f32[2048,6144]{1,0:T(8,128)}, f32[2048,2048]{1,0:T(8,128)})) %all-reduce.3.cloned.1.call-update) | async-done | bytes 67108880 | tf_op jit(solution)/shard_map/psum | solution.py:70
  2100.1 34.5 %copy.111 = f32[2048,6144]{1,0:T(8,128)} copy(f32[2048,6144]{1,0:T(8,128)} %get-tuple-element.36) | data formatting | bytes 100663296
  (67 shorter events, 309.5 us)
Async XLA Ops:
  12.9 62.6 %copy-start.7 = (f32[64,32]{1,0:T(8,128)}, f32[64,32]{1,0:T(8,128)S(1)}, u32[]{:S(2)}) copy-start(f32[64,32]{1,0:T(8,128)S(1)} %get-tuple-element.20) | copy-start | bytes 24580
  13.6 61.9 %copy-start.9 = (f32[2048]{0:T(1024)}, f32[2048]{0:T(1024)S(1)}, u32[]{:S(2)}) copy-start(f32[2048]{0:T(1024)S(1)} %convert_element_type.154) | copy-start | bytes 24580
  186.3 12.4 copy-start.11
  186.3 12.4 copy-start.12
  198.8 42.1 %copy-start.2 = (f32[32,128]{1,0:T(8,128)}, f32[32,128]{1,0:T(8,128)S(1)}, u32[]{:S(2)}) copy-start(f32[32,128]{1,0:T(8,128)S(1)} %get-tuple-element.33) | copy-start | bytes 49156
  198.8 42.1 %copy-start.4 = (f32[32,128]{1,0:T(8,128)}, f32[32,128]{1,0:T(8,128)S(1)}, u32[]{:S(2)}) copy-start(f32[32,128]{1,0:T(8,128)S(1)} %get-tuple-element.32) | copy-start | bytes 49156
  249.9 112.3 %all-to-all-start.2 = ((bf16[64,32,16,128]{3,1,0,2:T(8,128)(2,1)}), bf16[64,32,16,128]{3,1,0,2:T(8,128)(2,1)}, u32[]{:S(2)}, u32[]{:S(2)}) async-start(bf16[64,32,16,128]{3,1,0,2:T(8,128)(2,1)} %copy.62), calls=%async_computation.2 | async-start | bytes 16777216 | tf_op jit(solution)/shard_map/all_to_all | solution.py:45
  362.1 111.2 %all-to-all-start.1 = ((bf16[64,32,16,128]{3,1,0,2:T(8,128)(2,1)}), bf16[64,32,16,128]{3,1,0,2:T(8,128)(2,1)}, u32[]{:S(2)}, u32[]{:S(2)}) async-start(bf16[64,32,16,128]{3,1,0,2:T(8,128)(2,1)} %copy.59), calls=%async_computation.1 | async-start | bytes 16777216 | tf_op jit(solution)/shard_map/all_to_all | solution.py:44
  473.3 110.9 %all-to-all-start.4 = ((bf16[64,32,16,128]{3,1,0,2:T(8,128)(2,1)}), bf16[64,32,16,128]{3,1,0,2:T(8,128)(2,1)}, u32[]{:S(2)}, u32[]{:S(2)}) async-start(bf16[64,32,16,128]{3,1,0,2:T(8,128)(2,1)} %bitcast.162), calls=%async_computation.4 | async-start | bytes 16777216 | tf_op jit(solution)/shard_map/all_to_all | solution.py:58
  584.2 111.4 %all-to-all-start = ((bf16[64,32,16,128]{3,1,0,2:T(8,128)(2,1)}), bf16[64,32,16,128]{3,1,0,2:T(8,128)(2,1)}, u32[]{:S(2)}, u32[]{:S(2)}) async-start(bf16[64,32,16,128]{3,1,0,2:T(8,128)(2,1)} %bitcast.161), calls=%async_computation | async-start | bytes 16777216 | tf_op jit(solution)/shard_map/all_to_all | solution.py:46
  950.9 111.1 %all-to-all-start.6 = ((bf16[64,512,1,128]{3,0,2,1:T(8,128)(2,1)}), bf16[64,512,1,128]{3,0,2,1:T(8,128)(2,1)}, u32[]{:S(2)}, u32[]{:S(2)}) async-start(bf16[64,512,1,128]{3,0,2,1:T(8,128)(2,1)} %copy.77), calls=%async_computation.6 | async-start | bytes 16777216 | tf_op jit(solution)/shard_map/all_to_all | solution.py:65
  1062.1 110.9 %all-to-all-start.5 = ((bf16[64,512,1,128]{3,0,2,1:T(8,128)(2,1)}), bf16[64,512,1,128]{3,0,2,1:T(8,128)(2,1)}, u32[]{:S(2)}, u32[]{:S(2)}) async-start(bf16[64,512,1,128]{3,0,2,1:T(8,128)(2,1)} %copy.73), calls=%async_computation.5 | async-start | bytes 16777216 | tf_op jit(solution)/shard_map/all_to_all | solution.py:64
  1117.9 71.7 %copy-start.3 = (f32[32,128]{1,0:T(8,128)S(1)}, f32[32,128]{1,0:T(8,128)}, u32[]{:S(2)}) copy-start(f32[32,128]{1,0:T(8,128)} %copy-done.2) | copy-start | bytes 49156
  1173.0 111.3 %all-to-all-start.7 = ((bf16[64,512,1,128]{3,0,2,1:T(8,128)(2,1)}), bf16[64,512,1,128]{3,0,2,1:T(8,128)(2,1)}, u32[]{:S(2)}, u32[]{:S(2)}) async-start(bf16[64,512,1,128]{3,0,2,1:T(8,128)(2,1)} %copy.81), calls=%async_computation.7 | async-start | bytes 16777216 | tf_op jit(solution)/shard_map/all_to_all | solution.py:66
  1226.5 12.5 copy-start.5
  1284.4 161.0 %all-to-all-start.3 = ((bf16[64,512,1,128]{3,0,2,1:T(8,128)(2,1)}), bf16[64,512,1,128]{3,0,2,1:T(8,128)(2,1)}, u32[]{:S(2)}, u32[]{:S(2)}) async-start(bf16[64,512,1,128]{3,0,2,1:T(8,128)(2,1)} %copy.66), calls=%async_computation.3 | async-start | bytes 16777216 | tf_op jit(solution)/shard_map/all_to_all | solution.py:53
  1288.4 811.8 %all-reduce.3.cloned.1.call-start = ((), (), s32[]{:S(2)}) async-start(), calls=%async_computation.8 | async-start | bytes 134217728 | tf_op jit(solution)/shard_map/psum | solution.py:70
  1344.1 35.5 %copy-start.8 = (f32[64,32]{1,0:T(8,128)S(1)}, f32[64,32]{1,0:T(8,128)}, u32[]{:S(2)}) copy-start(f32[64,32]{1,0:T(8,128)} %copy-done.7) | copy-start | bytes 24580
  1344.1 35.5 %copy-start.10 = (f32[2048]{0:T(1024)S(1)}, f32[2048]{0:T(1024)}, u32[]{:S(2)}) copy-start(f32[2048]{0:T(1024)} %copy-done.9) | copy-start | bytes 24580
  1510.5 105.9 %copy-start.6 = (f32[64,32]{1,0:T(8,128)S(1)}, f32[64,32]{1,0:T(8,128)}, u32[]{:S(2)}) copy-start(f32[64,32]{1,0:T(8,128)} %get-tuple-element.19) | copy-start | bytes 24580
  1616.4 14.0 copy-start
  1616.4 16.1 copy-start.1
Sparse Core Ops, SparseCore 0:
  1510.7 589.4 all-reduce.2
where the time goes:
time: 2170 us; the launch traced here: 2150 us
  waiting for transfers between devices  905 us (42%)
  matrix products  560 us (26%)
  local copies, waits for them, and re-layouts  404 us (19%)
  other arithmetic  201 us (9%)
  starting transfers between devices  34.8 us (2%)
  blocking collectives  34.1 us (2%)
    psum x1, waiting for transfers between devices, device_step(): lax.psum(jnp.einsum('btd,bte->de', normed, d_proj, preferred_element_type...  445 us
    unnamed x30, local copies, waits for them, and re-layouts  98.5 us
    all_to_all x1, waiting for transfers between devices, device_step(): k_heads = to_heads(k_local)  97.9 us
    all_to_all x1, waiting for transfers between devices, device_step(): to_heads(d_attn.reshape(num_seqs, local_len, num_heads, head_dim))  88.8 us
    dot_general x1, matrix products, device_step(): jnp.einsum('bhqk,bqhd->bkhd', d_scores, q_heads, preferred_element_type=j...  85.9 us
    dot_general x1, matrix products, device_step(): jnp.einsum('bhqk,bkhd->bqhd', d_scores, k_heads, preferred_element_type=j...  85.7 us
    all_to_all x1, waiting for transfers between devices, device_step(): v_heads = to_heads(v_local)  78.8 us
    all_to_all x1, waiting for transfers between devices, device_step(): q_heads = to_heads(q_local)  74.3 us
  transfers between devices with their start and end apart: 9, of which 8 were waited for; matrix products, arithmetic and copies ran while one was open for 26% of the time, Pallas kernels for 0%

commit v1 on v0

v1 whole, which is shorter than its diff:
```python
import functools
import jax
import jax.numpy as jnp
from jax import lax
from jax.experimental import pallas as pl
from jax.experimental.pallas import tpu as pltpu
from jax.sharding import PartitionSpec as P

NORM_EPS = 1e-6
BF = jnp.bfloat16
F32 = jnp.float32
VMEM_LIMIT = 60 * 1024 * 1024


def dot_nn(a, b):
    return lax.dot_general(a, b, (((1,), (0,)), ((), ())), preferred_element_type=F32)


def dot_nt(a, b):
    return lax.dot_general(a, b, (((1,), (1,)), ((), ())), preferred_element_type=F32)


def rotate(u, cos, sin_signed):
    return u * cos + pltpu.roll(u, 64, 1) * sin_signed


def unrotate(u, cos, sin_signed):
    return u * cos - pltpu.roll(u, 64, 1) * sin_signed


def qkv_kernel(n_rot, n_tile, hidden_ref, gain_ref, w_ref, cos_ref, sin_ref, normed_t_ref, qkv_ref, normed_ref):
    n = pl.program_id(1)

    @pl.when(n == 0)
    def _():
        h = hidden_ref[...].astype(F32)
        inv = lax.rsqrt(jnp.mean(h * h, axis=-1, keepdims=True) + NORM_EPS)
        normed = (h * inv * gain_ref[...].astype(F32)).astype(BF)
        normed_ref[...] = normed
        normed_t_ref[...] = normed.T

    proj = dot_nn(normed_ref[...], w_ref[...])

    @pl.when(n < n_rot)
    def _():
        for h in range(n_tile // 128):
            cols = slice(h * 128, (h + 1) * 128)
            qkv_ref[0, :, cols] = rotate(proj[:, cols], cos_ref[...], sin_ref[...]).astype(BF)

    @pl.when(n >= n_rot)
    def _():
        qkv_ref[0] = proj.astype(BF)


def qkv_call(hidden, gain, w_qkv, cos, sin):
    rows, dim = hidden.shape
    seq = cos.shape[0]
    tile = 512
    per = dim // tile
    return pl.pallas_call(
        functools.partial(qkv_kernel, 2 * per, tile),
        grid=(rows // seq, 3 * per),
        in_specs=[
            pl.BlockSpec((seq, dim), lambda s, n: (s, 0)),
            pl.BlockSpec((1, dim), lambda s, n: (0, 0)),
            pl.BlockSpec((dim, tile), lambda s, n: (0, n)),
            pl.BlockSpec((seq, 128), lambda s, n: (0, 0)),
            pl.BlockSpec((seq, 128), lambda s, n: (0, 0)),
        ],
        out_specs=[
            pl.BlockSpec((dim, seq), lambda s, n: (0, s)),
            pl.BlockSpec((1, seq, tile), lambda s, n: (n // per, s, n % per)),
        ],
        out_shape=[
            jax.ShapeDtypeStruct((dim, rows), BF),
            jax.ShapeDtypeStruct((3, rows, dim), BF),
        ],
        scratch_shapes=[pltpu.VMEM((seq, dim), BF)],
        compiler_params=pltpu.CompilerParams(vmem_limit_bytes=VMEM_LIMIT),
        cost_estimate=pl.CostEstimate(flops=2 * rows * dim * 3 * dim, bytes_accessed=rows * dim * 10 + 6 * dim * dim, transcendentals=0),
        name="qkv",
    )(hidden, gain, w_qkv, cos, sin)


def nt_kernel(a_ref, b_ref, o_ref):
    o_ref[...] = dot_nt(a_ref[...], b_ref[...]).astype(BF)


def nt_call(a, b):
    rows, k = a.shape
    n = b.shape[0]
    tm, tn = 1024, 512
    return pl.pallas_call(
        nt_kernel,
        grid=(rows // tm, n // tn),
        in_specs=[pl.BlockSpec((tm, k), lambda i, j: (i, 0)), pl.BlockSpec((tn, k), lambda i, j: (j, 0))],
        out_specs=pl.BlockSpec((tm, tn), lambda i, j: (i, j)),
        out_shape=jax.ShapeDtypeStruct((rows, n), BF),
        compiler_params=pltpu.CompilerParams(vmem_limit_bytes=VMEM_LIMIT),
        cost_estimate=pl.CostEstimate(flops=2 * rows * n * k, bytes_accessed=2 * (rows * k + n * k + rows * n), transcendentals=0),
        name="d_attn",
    )(a, b)


def out_kernel(a_ref, b_ref, h_ref, o_ref):
    o_ref[...] = (h_ref[...].astype(F32) + dot_nn(a_ref[...], b_ref[...])).astype(BF)


def out_call(a, b, h):
    rows, k = a.shape
    n = b.shape[1]
    tm, tn = 1024, 512
    return pl.pallas_call(
        out_kernel,
        grid=(rows // tm, n // tn),
        in_specs=[
            pl.BlockSpec((tm, k), lambda i, j: (i, 0)),
            pl.BlockSpec((k, tn), lambda i, j: (0, j)),
            pl.BlockSpec((tm, tn), lambda i, j: (i, j)),
        ],
        out_specs=pl.BlockSpec((tm, tn), lambda i, j: (i, j)),
        out_shape=jax.ShapeDtypeStruct((rows, n), BF),
        compiler_params=pltpu.CompilerParams(vmem_limit_bytes=VMEM_LIMIT),
        cost_estimate=pl.CostEstimate(flops=2 * rows * n * k, bytes_accessed=2 * (rows * k + n * k + 2 * rows * n), transcendentals=0),
        name="out_proj",
    )(a, b, h)


def attn_kernel(heads, scale, qkv_ref, do_ref, cos_ref, sin_ref, o_ref, o_t_ref, dproj_ref):
    seq = qkv_ref.shape[1]
    blk = 256
    cos = cos_ref[...]
    sin = sin_ref[...]
    for h in range(heads):
        cols = slice(h * 128, (h + 1) * 128)
        q = qkv_ref[0, :, cols]
        k = qkv_ref[1, :, cols]
        v = qkv_ref[2, :, cols]
        do = do_ref[:, cols]
        k_t = k.T
        v_t = v.T
        dk = [None] * (seq // blk)
        dv = [None] * (seq // blk)
        dq_t = []
        o_t = []
        for j in range(seq // blk):
            end = (j + 1) * blk
            q_j = q[j * blk:end]
            do_j = do[j * blk:end]
            s = dot_nt(k[:end], q_j)
            row = lax.broadcasted_iota(jnp.int32, (end, blk), 0)
            col = lax.broadcasted_iota(jnp.int32, (end, blk), 1) + j * blk
            s = jnp.where(row <= col, s * scale, -1e30)
            m = jnp.max(s, axis=0, keepdims=True)
            e = jnp.exp(s - m)
            p = e * (1.0 / jnp.sum(e, axis=0, keepdims=True))
            p_bf = p.astype(BF)
            o_t.append(dot_nn(v_t[:, :end], p_bf))
            dp = dot_nt(v[:end], do_j).astype(BF).astype(F32)
            delta = jnp.sum(p * dp, axis=0, keepdims=True)
            ds = (p * (dp - delta) * scale).astype(BF)
            dv_j = dot_nn(p_bf, do_j)
            dk_j = dot_nn(ds, q_j)
            dq_t.append(dot_nn(k_t[:, :end], ds))
            for i in range(j + 1):
                part = slice(i * blk, (i + 1) * blk)
                dv[i] = dv_j[part] if dv[i] is None else dv[i] + dv_j[part]
                dk[i] = dk_j[part] if dk[i] is None else dk[i] + dk_j[part]
        for j in range(seq // blk):
            rows = slice(j * blk, (j + 1) * blk)
            o_ref[rows, cols] = o_t[j].T.astype(BF)
            o_t_ref[cols, rows] = o_t[j].astype(BF)
            dq_j = dq_t[j].T.astype(BF).astype(F32)
            dk_j = dk[j].astype(BF).astype(F32)
            dproj_ref[0, rows, cols] = unrotate(dq_j, cos[rows], sin[rows]).astype(BF)
            dproj_ref[1, rows, cols] = unrotate(dk_j, cos[rows], sin[rows]).astype(BF)
            dproj_ref[2, rows, cols] = dv[j].astype(BF)


def attn_call(qkv, d_attn, cos, sin):
    _, rows, dim = qkv.shape
    seq = cos.shape[0]
    heads = 2
    width = heads * 128
    return pl.pallas_call(
        functools.partial(attn_kernel, heads, 128 ** -0.5),
        grid=(rows // seq, dim // width),
        in_specs=[
            pl.BlockSpec((3, seq, width), lambda s, h: (0, s, h)),
            pl.BlockSpec((seq, width), lambda s, h: (s, h)),
            pl.BlockSpec((seq, 128), lambda s, h: (0, 0)),
            pl.BlockSpec((seq, 128), lambda s, h: (0, 0)),
        ],
        out_specs=[
            pl.BlockSpec((seq, width), lambda s, h: (s, h)),
            pl.BlockSpec((width, seq), lambda s, h: (h, s)),
            pl.BlockSpec((3, seq, width), lambda s, h: (0, s, h)),
        ],
        out_shape=[
            jax.ShapeDtypeStruct((rows, dim), BF),
            jax.ShapeDtypeStruct((dim, rows), BF),
            jax.ShapeDtypeStruct((3, rows, dim), BF),
        ],
        compiler_params=pltpu.CompilerParams(vmem_limit_bytes=VMEM_LIMIT),
        cost_estimate=pl.CostEstimate(flops=12 * rows * dim * seq, bytes_accessed=rows * dim * 16, transcendentals=rows * seq * 16),
        name="attention",
    )(qkv, d_attn, cos, sin)


MESH=pl.DeviceIdType.MESH
TW=256
PARTS=((0,384),(384,320),(704,320))
NS=3
NB=8

def reduce_kernel(n_qkv, n_all, at_hbm, ot_hbm, dproj_hbm, dout_hbm, g_hbm,
                  lhs, rhs, acc, r0, r1, r2, r3,
                  ld_sem, rhs_sem, s_send, s_recv, credit, loc_sem, g_send, g_recv):
    me=lax.axis_index('sp')
    dim=at_hbm.shape[0]
    core=me%2
    mate=me+1-2*core
    recv=(r0,r1,r2,r3)

    def link(d):
        w=2+d+d*d
        bit=(me//w)%2
        return bit, me+w*(1-2*bit)

    barrier=pltpu.get_barrier_semaphore()
    for p in (mate,link(0)[1],link(1)[1],link(2)[1]):
        pl.semaphore_signal(barrier,inc=1,device_id=(p,),device_id_type=MESH)
    pl.semaphore_wait(barrier,4)

    def dims(u,p,t):
        return (u+p+t-1)%3

    def offs(u,p,size):
        o=[0]
        for t in (1,2,3):
            b,_=link(dims(u,p,t))
            o.append(o[-1]+b*(size>>t))
        return o

    def half_rows(t):
        return (dim//2)>>t

    def rs_copies(u,t):
        sl=u%NS; nb=u%NB
        if t==0:
            return [pltpu.make_async_remote_copy(
                src_ref=acc.at[nb,pl.ds(pl.multiple_of((1-core)*(dim//2),dim//2),dim//2)],
                dst_ref=r0.at[sl],send_sem=s_send.at[0,sl],recv_sem=s_recv.at[0,sl],device_id=(mate,),device_id_type=MESH)]
        out=[]
        for p,(base,size) in enumerate(PARTS):
            o=offs(u,p,size)
            n=size>>t
            b,peer=link(dims(u,p,t))
            row=core*(dim//2)+base+o[t-1]+(1-b)*n
            out.append(pltpu.make_async_remote_copy(
                src_ref=acc.at[nb,pl.ds(pl.multiple_of(row,8),n)],
                dst_ref=recv[t].at[sl,pl.ds(base>>t,n)],
                send_sem=s_send.at[t,sl],recv_sem=s_recv.at[t,sl],device_id=(peer,),device_id_type=MESH))
        return out

    def all_rows(t,u):
        sl=u%NS
        return pltpu.make_async_remote_copy(src_ref=recv[t].at[sl],dst_ref=recv[t].at[sl],
            send_sem=s_send.at[t,sl],recv_sem=s_recv.at[t,sl],device_id=(mate,),device_id_type=MESH)

    def rs_start(u,t):
        sl=u%NS
        peers=[mate] if t==0 else [link(dims(u,p,t))[1] for p in range(3)]
        @pl.when(u>=NS)
        def _():
            pl.semaphore_wait(credit.at[t,sl],len(peers))
            all_rows(t,u).wait_send()
        for c in rs_copies(u,t): c.start()

    def rs_finish(u,t):
        sl=u%NS; nb=u%NB
        all_rows(t,u).wait_recv()
        if t==0:
            rows=pl.ds(pl.multiple_of(core*(dim//2),dim//2),dim//2)
            acc[nb,rows]=acc[nb,rows]+r0[sl]
            pl.semaphore_signal(credit.at[0,sl],inc=1,device_id=(mate,),device_id_type=MESH)
        else:
            for p,(base,size) in enumerate(PARTS):
                o=offs(u,p,size)
                n=size>>t
                rows=pl.ds(pl.multiple_of(core*(dim//2)+base+o[t],8),n)
                acc[nb,rows]=acc[nb,rows]+recv[t][sl,pl.ds(base>>t,n)]
                pl.semaphore_signal(credit.at[t,sl],inc=1,device_id=(link(dims(u,p,t))[1],),device_id_type=MESH)

    def g_at(u,row,n):
        return g_hbm.at[pl.ds(pl.multiple_of(row,8),n),pl.ds(pl.multiple_of(u*TW,TW),TW)]

    def ag_copies(u,t):
        if t==0:
            r=g_at(u,core*(dim//2),dim//2)
            return [pltpu.make_async_remote_copy(src_ref=r,dst_ref=r,send_sem=g_send.at[0,u%NS],recv_sem=g_recv.at[0,u],device_id=(mate,),device_id_type=MESH)]
        out=[]
        for p,(base,size) in enumerate(PARTS):
            o=offs(u,p,size)
            n=size>>t
            row=core*(dim//2)+base+o[t]
            _,peer=link(dims(u,p,t))
            dst=g_at(u,row,n)
            src=acc.at[u%NB,pl.ds(pl.multiple_of(row,8),n)] if t==3 else dst
            out.append(pltpu.make_async_remote_copy(src_ref=src,dst_ref=dst,send_sem=g_send.at[t,u%NS],recv_sem=g_recv.at[t,u],device_id=(peer,),device_id_type=MESH))
        return out

    def ag_rows(t,u):
        r=g_hbm.at[pl.ds(0,half_rows(t)),pl.ds(0,TW)]
        return pltpu.make_async_remote_copy(src_ref=r,dst_ref=r,send_sem=g_send.at[t,u%NS],recv_sem=g_recv.at[t,u],device_id=(mate,),device_id_type=MESH)

    def ag_start(u,t):
        @pl.when(u>=NS)
        def _():
            ag_rows(t,u).wait_send()
        for c in ag_copies(u,t): c.start()

    def local_copies(u):
        out=[]
        for p,(base,size) in enumerate(PARTS):
            o=offs(u,p,size)
            n=size>>3
            row=core*(dim//2)+base+o[3]
            out.append(pltpu.make_async_copy(acc.at[u%NB,pl.ds(pl.multiple_of(row,8),n)],g_at(u,row,n),loc_sem.at[u%NS]))
        return out

    def local_wait(u):
        pltpu.make_async_copy(acc.at[0,pl.ds(0,half_rows(3))],g_hbm.at[pl.ds(0,half_rows(3)),pl.ds(0,TW)],loc_sem.at[u%NS]).wait()

    def rhs_start(u):
        per=dim//TW
        @pl.when(u<n_qkv)
        def _():
            pltpu.make_async_copy(dproj_hbm.at[u//per,:,pl.ds(pl.multiple_of((u%per)*TW,TW),TW)],rhs.at[u%2],rhs_sem.at[u%2]).start()
        @pl.when(u>=n_qkv)
        def _():
            pltpu.make_async_copy(dout_hbm.at[:,pl.ds(pl.multiple_of((u-n_qkv)*TW,TW),TW)],rhs.at[u%2],rhs_sem.at[u%2]).start()

    def rhs_wait(u):
        pltpu.make_async_copy(dout_hbm.at[:,pl.ds(0,TW)],rhs.at[u%2],rhs_sem.at[u%2]).wait()

    pltpu.make_async_copy(at_hbm,lhs.at[0],ld_sem.at[0]).start()
    pltpu.make_async_copy(ot_hbm,lhs.at[1],ld_sem.at[1]).start()
    rhs_start(0)
    pltpu.make_async_copy(at_hbm,lhs.at[0],ld_sem.at[0]).wait()
    pltpu.make_async_copy(ot_hbm,lhs.at[1],ld_sem.at[1]).wait()

    def guarded(u,fn):
        @pl.when(jnp.logical_and(u>=0,u<n_all))
        def _(): fn()

    def step(i,carry):
        def ag0(u):
            ag_rows(0,u).wait_recv()
        def ag1(u):
            ag_rows(1,u).wait_recv(); ag_start(u,0)
        def ag2(u):
            ag_rows(2,u).wait_recv(); ag_start(u,1)
        def ag3(u):
            ag_rows(3,u).wait_recv(); local_wait(u); ag_start(u,2)
        def last(u):
            rs_finish(u,3)
            for c in local_copies(u): c.start()
            ag_start(u,3)
        def mid(t):
            def f(u):
                rs_finish(u,t); rs_start(u,t+1)
            return f
        def first(u):
            @pl.when(u+1<n_all)
            def _(): rhs_start(u+1)
            rhs_wait(u)
            which=jnp.where(u<n_qkv,0,1)
            @pl.loop(0,dim//512)
            def _(b):
                rows=pl.ds(pl.multiple_of(b*512,512),512)
                acc[u%NB,rows]=dot_nn(lhs[which,rows],rhs[u%2])
            rs_start(u,0)
        for lag,fn in ((1,mid(0)),(2,mid(1)),(3,mid(2)),(4,last),(5,ag3),(6,ag2),(7,ag1),(8,ag0),(0,first)):
            guarded(i-lag,functools.partial(fn,i-lag))
        return carry
    lax.fori_loop(0,n_all+8,step,0)

    for j in range(NS):
        u=n_all-NS+j
        for t in range(4):
            all_rows(t,u).wait_send()
            pl.semaphore_wait(credit.at[t,u%NS],1 if t==0 else 3)
            ag_rows(t,u).wait_send()

def reduce_call(at,ot,dproj,dout):
    dim=at.shape[0]; rows=at.shape[1]
    n_qkv=3*dim//TW; n_all=4*dim//TW
    any_=pl.BlockSpec(memory_space=pl.ANY)
    h=dim//2
    D=pltpu.SemaphoreType.DMA
    return pl.pallas_call(
        functools.partial(reduce_kernel,n_qkv,n_all),
        in_specs=[any_]*4,out_specs=any_,
        out_shape=jax.ShapeDtypeStruct((dim,4*dim),F32),
        scratch_shapes=[pltpu.VMEM((2,dim,rows),BF),pltpu.VMEM((2,rows,TW),BF),pltpu.VMEM((NB,dim,TW),F32),
            pltpu.VMEM((NS,h,TW),F32),pltpu.VMEM((NS,h>>1,TW),F32),pltpu.VMEM((NS,h>>2,TW),F32),pltpu.VMEM((NS,h>>3,TW),F32),
            D((2,)),D((2,)),D((4,NS)),D((4,NS)),pltpu.SemaphoreType.REGULAR((4,NS)),D((NS,)),D((4,NS)),D((4,n_all))],
        compiler_params=pltpu.CompilerParams(collective_id=1,has_side_effects=True,vmem_limit_bytes=62<<20),
        cost_estimate=pl.CostEstimate(flops=8*rows*dim*dim,bytes_accessed=40*dim*dim,transcendentals=0),
        name="reduce",
    )(at,ot,dproj,dout)


def dh_kernel(steps, dproj_ref, w_ref, hidden_ref, dout_ref, gain_ref, dh_ref, dgain_ref, acc_ref):
    s, n = pl.program_id(0), pl.program_id(1)
    part = dot_nt(dproj_ref[0], w_ref[...])

    @pl.when(n == 0)
    def _():
        acc_ref[...] = part

    @pl.when(n > 0)
    def _():
        acc_ref[...] += part

    @pl.when(n == steps - 1)
    def _():
        h = hidden_ref[...].astype(F32)
        inv = lax.rsqrt(jnp.mean(h * h, axis=-1, keepdims=True) + NORM_EPS)
        dn = acc_ref[...].astype(BF).astype(F32)
        dgain = jnp.sum(dn * h * inv, axis=0, keepdims=True)
        ds = dn * gain_ref[...].astype(F32)
        dh = dout_ref[...].astype(F32) + inv * ds - h * (inv * inv * inv) * jnp.mean(ds * h, axis=-1, keepdims=True)
        dh_ref[...] = dh.astype(BF)

        @pl.when(s == 0)
        def _():
            dgain_ref[...] = dgain

        @pl.when(s > 0)
        def _():
            dgain_ref[...] += dgain


def dh_call(dproj, w_qkv, hidden, d_out, gain):
    rows, dim = hidden.shape
    tm, tk = 512, 1024
    per = dim // tk
    return pl.pallas_call(
        functools.partial(dh_kernel, 3 * per),
        grid=(rows // tm, 3 * per),
        in_specs=[
            pl.BlockSpec((1, tm, tk), lambda s, n: (n // per, s, n % per)),
            pl.BlockSpec((dim, tk), lambda s, n: (0, n)),
            pl.BlockSpec((tm, dim), lambda s, n: (s, 0)),
            pl.BlockSpec((tm, dim), lambda s, n: (s, 0)),
            pl.BlockSpec((1, dim), lambda s, n: (0, 0)),
        ],
        out_specs=[
            pl.BlockSpec((tm, dim), lambda s, n: (s, 0)),
            pl.BlockSpec((1, dim), lambda s, n: (0, 0)),
        ],
        out_shape=[jax.ShapeDtypeStruct((rows, dim), BF), jax.ShapeDtypeStruct((1, dim), F32)],
        scratch_shapes=[pltpu.VMEM((tm, dim), F32)],
        compiler_params=pltpu.CompilerParams(vmem_limit_bytes=VMEM_LIMIT),
        cost_estimate=pl.CostEstimate(flops=6 * rows * dim * dim, bytes_accessed=rows * dim * 14 + 6 * dim * dim, transcendentals=0),
        name="d_hidden",
    )(dproj, w_qkv, hidden, d_out, gain)


def solution(mesh):
    group = mesh.shape['sp']
    token_spec = P(None, 'sp', None)
    table_spec = P('sp', None)
    swap = functools.partial(lax.all_to_all, axis_name='sp', split_axis=0, concat_axis=0, tiled=True)

    def device_step(hidden, norm_gain, w_qkv, w_out, cos_tab, sin_tab, d_out):
        num_seqs, local_len, dim = hidden.shape
        mine = num_seqs // group
        seq = local_len * group
        rows = mine * seq

        def to_seqs(x):
            x = x.reshape(mine, group, local_len, dim)
            x = lax.all_to_all(x, 'sp', split_axis=1, concat_axis=1, tiled=True)
            return x.reshape(rows, dim)

        def to_tokens(x):
            x = x.reshape(mine, group, local_len, dim)
            x = lax.all_to_all(x, 'sp', split_axis=1, concat_axis=1, tiled=True)
            return x.reshape(num_seqs, local_len, dim)

        tab = lax.all_gather(jnp.concatenate([cos_tab, sin_tab], axis=1), 'sp', axis=0, tiled=True)
        cos, sin = tab[:, :64], tab[:, 64:]
        cos = jnp.concatenate([cos, cos], axis=1)
        sin = jnp.concatenate([-sin, sin], axis=1)
        gain = norm_gain.reshape(1, dim)

        h_seq = to_seqs(hidden)
        normed_t, qkv = qkv_call(h_seq, gain, w_qkv, cos, sin)
        do_seq = to_seqs(d_out)
        d_attn = nt_call(do_seq, w_out)
        attn, attn_t, dproj = attn_call(qkv, d_attn, cos, sin)
        y = to_tokens(out_call(attn, w_out, h_seq))
        dw = reduce_call(normed_t, attn_t, dproj, do_seq)
        dh, dgain = dh_call(dproj, w_qkv, h_seq, do_seq, gain)
        dh = to_tokens(dh)
        dgain = lax.psum(dgain, 'sp')
        return y, dh, dw[:, :3 * dim], dw[:, 3 * dim:], dgain.reshape(dim)

    return jax.shard_map(device_step, mesh=mesh, in_specs=(token_spec, P(None), P(None, None), P(None, None), table_spec, table_spec, token_spec), out_specs=(token_spec, token_spec, P(None, None), P(None, None), P(None)), check_vma=False)
```

time: 2170 us -> 1330 us (0.61)
  Pallas kernels: 0 us -> 876 us
  waiting for transfers between devices: 905 us -> 173 us
  matrix products: 560 us -> 0 us
  local copies, waits for them, and re-layouts: 404 us -> 114 us
  other arithmetic: 201 us -> 1.21 us
  blocking collectives: 34.1 us -> 147 us
    pallas_call x0 -> x6, Pallas kernels: none -> 876 us  [the longest x1 536 us: reduce_call(): pl.pallas_call(functools.partial(reduce_kernel, n_qkv, n_all), in_specs=[...]
    dot_general x11 -> x0, matrix products: 527 us -> none  [the longest x1 85.9 us: device_step(): jnp.einsum('bhqk,bqhd->bkhd', d_scores, q_heads, preferred_element_type=j...]
    psum x1 -> x0, waiting for transfers between devices: 445 us -> none  [device_step(): lax.psum(jnp.einsum('btd,bte->de', normed, d_proj, preferred_element_type...]
    all_to_all x8 -> x4, waiting for transfers between devices: 460 us -> 173 us  [the longest x2 98.5 us: to_seqs(): x = lax.all_to_all(x, 'sp', split_axis=1, concat_axis=1, tiled=True)]
    all_gather x0 -> x1, blocking collectives: none -> 116 us  [device_step(): lax.all_gather(jnp.concatenate([cos_tab, sin_tab], axis=1), 'sp', axis=0,...]
    unnamed x30 -> x8, local copies, waits for them, and re-layouts: 98.5 us -> 0.01 us
    convert_element_type x4 -> x0, other arithmetic: 91.6 us -> none  [the longest x1 42.1 us: device_step(): (projected[:, :, 1] * cos_full + rotate_half(projected[:, :, 1]) * sin_fu...]
    all_to_all x9 -> x4, local copies, waits for them, and re-layouts: 101 us -> 33.8 us  [the longest x2 16.9 us: to_tokens(): x = lax.all_to_all(x, 'sp', split_axis=1, concat_axis=1, tiled=True)]
  transfers between devices with their start and end apart: 9 -> 4, of which waited for: 8 -> 2; matrix products, arithmetic and copies ran while one was open for 26% -> 6% of each run, Pallas kernels for 0% -> 44%
where the time goes in v1:
time: 1330 us
  Pallas kernels  876 us (66%)
  waiting for transfers between devices  173 us (13%)
  blocking collectives  147 us (11%)
  local copies, waits for them, and re-layouts  114 us (9%)
  starting transfers between devices  16.6 us (1%)
    pallas_call x1, Pallas kernels, reduce_call(): pl.pallas_call(functools.partial(reduce_kernel, n_qkv, n_all), in_specs=[...  536 us
    all_gather x1, blocking collectives, device_step(): lax.all_gather(jnp.concatenate([cos_tab, sin_tab], axis=1), 'sp', axis=0,...  116 us
    pallas_call x1, Pallas kernels, attn_call(): pl.pallas_call(functools.partial(attn_kernel, heads, 128 ** (-0.5)), grid...  112 us
    all_to_all x2, waiting for transfers between devices, to_seqs(): x = lax.all_to_all(x, 'sp', split_axis=1, concat_axis=1, tiled=True)  98.5 us
    pallas_call x1, Pallas kernels, dh_call(): pl.pallas_call(functools.partial(dh_kernel, 3 * per), grid=(rows // tm, 3...  91.1 us
    pallas_call x1, Pallas kernels, qkv_call(): pl.pallas_call(functools.partial(qkv_kernel, 2 * per, tile), grid=(rows /...  89.3 us
    all_to_all x2, waiting for transfers between devices, to_tokens(): x = lax.all_to_all(x, 'sp', split_axis=1, concat_axis=1, tiled=True)  74.6 us
    slice x2, local copies, waits for them, and re-layouts, device_step(): return (y, dh, dw[:, :3 * dim], dw[:, 3 * dim:], dgain.reshape(dim))  46.3 us
  transfers between devices with their start and end apart: 4, of which 2 were waited for; matrix products, arithmetic and copies ran while one was open for 6% of the time, Pallas kernels for 44%

profile of v1, /device:TPU:0, one launch (start us, length us, event | category | flops | bytes accessed | tf_op | source)
XLA Modules:
  0.0 1329.5 jit_solution(4850615344977005034)
XLA Ops:
  0.6 8.4 copy.18
  9.1 5.3 all-to-all-start.1
  14.4 8.4 copy.16
  22.9 98.5 %all-to-all-done.1 = bf16[4,16,32,2048]{3,2,0,1:T(8,128)(2,1)} async-done(((bf16[4,16,32,2048]{3,2,0,1:T(8,128)(2,1)}), bf16[4,16,32,2048]{3,2,0,1:T(8,128)(2,1)}, u32[]{:S(2)}, u32[]{:S(2)}) %all-to-all-start.1) | async-done | bytes 8388640 | tf_op jit(solution)/shard_map/all_to_all | solution.py:486
  121.4 4.0 all-to-all-start
  125.4 0.0 copy-done.3
  125.4 0.6 reshape.42.gain_ref
  126.0 0.1 pad_maximum_fusion.2
  126.1 115.6 %all_gather.3 = f32[512,128]{1,0:T(8,128)S(1)} all-gather(f32[32,128]{1,0:T(8,128)S(1)} %pad_maximum_fusion.2), channel_id=1, replica_groups=mesh['sp'=16] {'sp'}, dimensions={0}, use_global_device_ids=true | all-gather | bytes 278528 | tf_op jit(solution)/shard_map/all_gather | solution.py:494
  241.6 0.1 slice_negate_fusion
  241.8 1.0 pad_maximum_fusion
  242.8 8.4 copy.19
  251.2 23.8 %d_attn.1.do_ref = bf16[2048,2048]{1,0:T(8,128)(2,1)} custom-call(bf16[2048,2048]{1,0:T(8,128)(2,1)} %bitcast.11, bf16[2048,2048]{1,0:T(8,128)(2,1)} %b_ref.3), custom_call_target="tpu_custom_call" | custom-call | flops 17179869184 | bytes 25165824 | tf_op jit(solution)/shard_map/d_attn/pallas_call | solution.py:93
  275.0 0.0 all-to-all-done
  275.0 8.4 copy.17
  283.5 89.3 %qkv.1 = (bf16[2048,2048]{1,0:T(8,128)(2,1)}, bf16[3,2048,2048]{2,1,0:T(8,128)(2,1)}) custom-call(bf16[2048,2048]{1,0:T(8,128)(2,1)} %bitcast.14, bf16[1,2048]{1,0:T(2,128)(2,1)} %reshape.42.gain_ref, bf16[2048,6144]{1,0:T(8,128)(2,1)} %w_ref.3, f32[512,128]{1,0:T(8,128)} %get-tuple-element.22.cos_ref, f32[512,128]{1,0:T(8,128)} %get-tuple-element.23.sin_ref), custom_call_target="tpu_custom_call" | custom-call | flops 51539607552 | bytes 67108864 | tf_op jit(solution)/shard_map/qkv/pallas_call | solution.py:60
  372.8 112.3 %attention.1 = (bf16[2048,2048]{1,0:T(8,128)(2,1)}, bf16[2048,2048]{1,0:T(8,128)(2,1)}, bf16[3,2048,2048]{2,1,0:T(8,128)(2,1)}) custom-call(bf16[3,2048,2048]{2,1,0:T(8,128)(2,1)} %get-tuple-element.12.qkv_ref, bf16[2048,2048]{1,0:T(8,128)(2,1)} %d_attn.1.do_ref, f32[512,128]{1,0:T(8,128)} %get-tuple-element.22.cos_ref, f32[512,128]{1,0:T(8,128)} %get-tuple-element.23.sin_ref), custom_call_target="tpu_custom_call" | custom-call | flops 25769803776 | bytes 67108864 | tf_op jit(solution)/shard_map/attention/pallas_call | solution.py:185
  485.0 91.1 %d_hidden.1 = (bf16[2048,2048]{1,0:T(8,128)(2,1)}, f32[1,2048]{1,0:T(1,128)}) custom-call(bf16[3,2048,2048]{2,1,0:T(8,128)(2,1)} %get-tuple-element.14.dproj_ref.dproj_hbm, bf16[2048,6144]{1,0:T(8,128)(2,1)} %w_ref.3, bf16[2048,2048]{1,0:T(8,128)(2,1)} %bitcast.15, bf16[2048,2048]{1,0:T(8,128)(2,1)} %bitcast.12, bf16[1,2048]{1,0:T(2,128)(2,1)} %reshape.42.gain_ref), custom_call_target="tpu_custom_call" | custom-call | flops 51539607552 | bytes 83886080 | tf_op jit(solution)/shard_map/d_hidden/pallas_call | solution.py:450
  576.1 8.3 copy.22
  584.3 3.5 all-to-all-start.3
  587.8 24.4 %out_proj.1 = bf16[2048,2048]{1,0:T(8,128)(2,1)} custom-call(bf16[2048,2048]{1,0:T(8,128)(2,1)} %get-tuple-element.13.a_ref, bf16[2048,2048]{1,0:T(8,128)(2,1)} %b_ref.3, bf16[2048,2048]{1,0:T(8,128)(2,1)} %bitcast.16), custom_call_target="tpu_custom_call" | custom-call | flops 17179869184 | bytes 33554432 | tf_op jit(solution)/shard_map/out_proj/pallas_call | solution.py:113
  612.2 8.2 copy.20
  620.5 74.6 %all-to-all-done.3 = bf16[4,16,32,2048]{3,2,0,1:T(8,128)(2,1)} async-done(((bf16[4,16,32,2048]{3,2,0,1:T(8,128)(2,1)}), bf16[4,16,32,2048]{3,2,0,1:T(8,128)(2,1)}, u32[]{:S(2)}, u32[]{:S(2)}) %all-to-all-start.3) | async-done | bytes 8388640 | tf_op jit(solution)/shard_map/all_to_all | solution.py:491
  695.1 3.8 all-to-all-start.2
  698.9 535.6 %reduce.1 = f32[2048,8192]{1,0:T(8,128)} custom-call(bf16[2048,2048]{1,0:T(8,128)(2,1)} %get-tuple-element.16.at_hbm, bf16[2048,2048]{1,0:T(8,128)(2,1)} %get-tuple-element.17.ot_hbm, bf16[3,2048,2048]{2,1,0:T(8,128)(2,1)} %get-tuple-element.14.dproj_ref.dproj_hbm, bf16[2048,2048]{1,0:T(8,128)(2,1)} %bitcast.13), custom_call_target="tpu_custom_call" | custom-call | flops 68719476736 | bytes 167772160 | tf_op jit(solution)/shard_map/reduce/pallas_call | solution.py:402
  1234.5 11.8 slice.15
  1246.3 34.5 %slice.14 = f32[2048,6144]{1,0:T(8,128)} slice(f32[2048,8192]{1,0:T(8,128)} %reduce.1), slice={[0:2048], [0:6144]} | slice | bytes 100663296 | tf_op jit(solution)/shard_map/slice | solution.py:510
  1280.8 0.0 copy-done.2
  1280.8 31.8 %psum.7 = f32[2048]{0:T(1024)} all-reduce(f32[2048]{0:T(1024)S(1)} %bitcast.21), channel_id=1, replica_groups=mesh['sp'=16] {'sp'}, use_global_device_ids=true, to_apply=%region_0.0 | all-reduce | flops 2048 | bytes 16384 | tf_op jit(solution)/shard_map/psum | solution.py:509
  1312.6 8.4 copy.23
  1321.1 0.0 all-to-all-done.2
  1321.1 8.4 copy.21
  (6 shorter events, 0.0 us)
Async XLA Ops:
  9.1 112.3 %all-to-all-start.1 = ((bf16[4,16,32,2048]{3,2,0,1:T(8,128)(2,1)}), bf16[4,16,32,2048]{3,2,0,1:T(8,128)(2,1)}, u32[]{:S(2)}, u32[]{:S(2)}) async-start(bf16[4,16,32,2048]{3,2,0,1:T(8,128)(2,1)} %copy.18), calls=%async_computation.1 | async-start | bytes 16777216 | tf_op jit(solution)/shard_map/all_to_all | solution.py:486
  22.9 102.5 %copy-start.3 = (bf16[2048]{0:T(1024)(128)(2,1)S(1)}, bf16[2048]{0:T(1024)(128)(2,1)}, u32[]{:S(2)}) copy-start(bf16[2048]{0:T(1024)(128)(2,1)} %param.8) | copy-start | bytes 12292
  22.9 103.1 %copy-start = (f32[32,64]{1,0:T(8,128)S(1)}, f32[32,64]{1,0:T(8,128)}, u32[]{:S(2)}) copy-start(f32[32,64]{1,0:T(8,128)} %param.12) | copy-start | bytes 24580
  22.9 103.1 %copy-start.1 = (f32[32,64]{1,0:T(8,128)S(1)}, f32[32,64]{1,0:T(8,128)}, u32[]{:S(2)}) copy-start(f32[32,64]{1,0:T(8,128)} %param.11) | copy-start | bytes 24580
  121.4 153.7 %all-to-all-start = ((bf16[4,16,32,2048]{3,2,0,1:T(8,128)(2,1)}), bf16[4,16,32,2048]{3,2,0,1:T(8,128)(2,1)}, u32[]{:S(2)}, u32[]{:S(2)}) async-start(bf16[4,16,32,2048]{3,2,0,1:T(8,128)(2,1)} %copy.16), calls=%async_computation | async-start | bytes 16777216 | tf_op jit(solution)/shard_map/all_to_all | solution.py:486
  584.3 110.7 %all-to-all-start.3 = ((bf16[4,16,32,2048]{3,2,0,1:T(8,128)(2,1)}), bf16[4,16,32,2048]{3,2,0,1:T(8,128)(2,1)}, u32[]{:S(2)}, u32[]{:S(2)}) async-start(bf16[4,16,32,2048]{3,2,0,1:T(8,128)(2,1)} %copy.22), calls=%async_computation.3 | async-start | bytes 16777216 | tf_op jit(solution)/shard_map/all_to_all | solution.py:491
  695.1 626.0 %all-to-all-start.2 = ((bf16[4,16,32,2048]{3,2,0,1:T(8,128)(2,1)}), bf16[4,16,32,2048]{3,2,0,1:T(8,128)(2,1)}, u32[]{:S(2)}, u32[]{:S(2)}) async-start(bf16[4,16,32,2048]{3,2,0,1:T(8,128)(2,1)} %copy.20), calls=%async_computation.2 | async-start | bytes 16777216 | tf_op jit(solution)/shard_map/all_to_all | solution.py:491
  1246.3 34.5 %copy-start.2 = (f32[1,2048]{1,0:T(1,128)S(1)}, f32[1,2048]{1,0:T(1,128)}, u32[]{:S(2)}) copy-start(f32[1,2048]{1,0:T(1,128)} %get-tuple-element.18) | copy-start | bytes 24580

commit v2 on v0

v2 whole, which is shorter than its diff:
```python
import functools
import jax
import jax.numpy as jnp
from jax import lax
from jax.experimental import pallas as pl
from jax.experimental.pallas import tpu as pltpu
from jax.sharding import PartitionSpec as P

NORM_EPS = 1e-6
BF = jnp.bfloat16
F32 = jnp.float32
VMEM_LIMIT = 60 * 1024 * 1024


def dot_nn(a, b):
    return lax.dot_general(a, b, (((1,), (0,)), ((), ())), preferred_element_type=F32)


def dot_nt(a, b):
    return lax.dot_general(a, b, (((1,), (1,)), ((), ())), preferred_element_type=F32)


def rotate(u, cos, sin_signed):
    return u * cos + pltpu.roll(u, 64, 1) * sin_signed


def unrotate(u, cos, sin_signed):
    return u * cos - pltpu.roll(u, 64, 1) * sin_signed


MESH = pl.DeviceIdType.MESH


def flipped(me,j):
    p=me
    for b in range(4):
        if (j>>b)&1:
            p=p+(1<<b)*(1-2*((me//(1<<b))%2))
    return p

ORDER=(2,4,8,1,3,5,9,6,10,12,7,11,13,14,15)

def exchange_kernel(hidden, d_out, tab, gain_ref, w_qkv, w_out,
                    h_seq, do_seq, tab_all, a_t, qkv, d_attn,
                    own, own_tab, hbuf, normed, normed_t, tabs,
                    h_send, h_recv, d_send, d_recv, t_send, t_recv, own_sem, ld_sem, at_sem):
    me=lax.axis_index('sp')
    group=16
    seqs=hidden.shape[0]//group
    loc=hidden.shape[1]
    dim=hidden.shape[2]
    seq=loc*group
    barrier=pltpu.get_barrier_semaphore()
    for j in range(1,group):
        pl.semaphore_signal(barrier,inc=1,device_id=(flipped(me,j),),device_id_type=MESH)
    pl.semaphore_wait(barrier,group-1)

    for j in ORDER:
        pltpu.make_async_remote_copy(src_ref=tab,dst_ref=tab_all.at[pl.ds(pl.multiple_of(me*loc,loc),loc)],send_sem=t_send,recv_sem=t_recv,
            device_id=(flipped(me,j),),device_id_type=MESH).start()
    def send(src,dst,ss,rs,c):
        for j in ORDER:
            peer=flipped(me,j)
            pltpu.make_async_remote_copy(src_ref=src.at[peer*seqs+c],
                dst_ref=dst.at[pl.ds(pl.multiple_of(c*seq+me*loc,loc),loc)],
                send_sem=ss.at[c],recv_sem=rs.at[c],device_id=(peer,),device_id_type=MESH).start()
    for c in range(seqs): send(hidden,h_seq,h_send,h_recv,c)
    for c in range(seqs): send(d_out,do_seq,d_send,d_recv,c)

    copies=[]
    for c in range(seqs):
        copies.append((hidden.at[me*seqs+c],own.at[c],h_seq.at[pl.ds(pl.multiple_of(c*seq+me*loc,loc),loc)]))
        copies.append((d_out.at[me*seqs+c],own.at[seqs+c],do_seq.at[pl.ds(pl.multiple_of(c*seq+me*loc,loc),loc)]))
    copies.append((tab,own_tab,tab_all.at[pl.ds(pl.multiple_of(me*loc,loc),loc)]))
    for n,(a,b,_) in enumerate(copies): pltpu.make_async_copy(a,b,own_sem.at[n]).start()
    for n,(a,b,d) in enumerate(copies):
        pltpu.make_async_copy(a,b,own_sem.at[n]).wait()
        pltpu.make_async_copy(b,d,own_sem.at[n]).start()
    for n,(a,b,d) in enumerate(copies):
        pltpu.make_async_copy(b,d,own_sem.at[n]).wait()

    def from_all(dst,ss,rs):
        r=dst.at[pl.ds(0,(group-1)*loc)]
        return pltpu.make_async_remote_copy(src_ref=r,dst_ref=r,send_sem=ss,recv_sem=rs,device_id=(flipped(me,1),),device_id_type=MESH)

    from_all(tab_all,t_send,t_recv).wait_recv()
    cp=pltpu.make_async_copy(tab_all,tabs,ld_sem); cp.start(); cp.wait()

    tile=512
    per=dim//tile
    def chunk(c,carry):
        rows=pl.ds(pl.multiple_of(c*seq,seq),seq)
        from_all(h_seq,h_send.at[c],h_recv.at[c]).wait_recv()
        cp=pltpu.make_async_copy(h_seq.at[rows],hbuf,ld_sem); cp.start(); cp.wait()
        @pl.when(c>0)
        def _():
            pltpu.make_async_copy(normed_t,a_t.at[:,rows],at_sem).wait()
        blk=128
        @pl.loop(0,seq//blk)
        def _(b):
            r=pl.ds(pl.multiple_of(b*blk,blk),blk)
            h=hbuf[r].astype(F32)
            inv=lax.rsqrt(jnp.mean(h*h,axis=-1,keepdims=True)+NORM_EPS)
            n=(h*inv*gain_ref[...].astype(F32)).astype(BF)
            normed[r]=n
            normed_t[:,r]=n.T
        pltpu.make_async_copy(normed_t,a_t.at[:,rows],at_sem).start()

        def body(w_ref,out_ref):
            n=pl.program_id(0)
            proj=dot_nn(normed[...],w_ref[...])
            @pl.when(n<2*per)
            def _():
                for h in range(tile//128):
                    cols=slice(h*128,(h+1)*128)
                    out_ref[0,:,cols]=rotate(proj[:,cols],tabs[:,:128],tabs[:,128:]).astype(BF)
            @pl.when(n>=2*per)
            def _():
                out_ref[0]=proj.astype(BF)
        pltpu.emit_pipeline(body,grid=(3*per,),
            in_specs=[pl.BlockSpec((dim,tile),lambda n:(0,n))],
            out_specs=[pl.BlockSpec((1,seq,tile),lambda n:(n//per,0,n%per))])(w_qkv,qkv.at[:,rows])
        return carry
    lax.fori_loop(0,seqs,chunk,0)

    def chunk2(c,carry):
        rows=pl.ds(pl.multiple_of(c*seq,seq),seq)
        from_all(do_seq,d_send.at[c],d_recv.at[c]).wait_recv()
        cp=pltpu.make_async_copy(do_seq.at[rows],hbuf,ld_sem); cp.start(); cp.wait()
        def body(w_ref,out_ref):
            out_ref[...]=dot_nt(hbuf[...],w_ref[...]).astype(BF)
        pltpu.emit_pipeline(body,grid=(per,),
            in_specs=[pl.BlockSpec((tile,dim),lambda n:(n,0))],
            out_specs=[pl.BlockSpec((seq,tile),lambda n:(0,n))])(w_out,d_attn.at[rows])
        return carry
    lax.fori_loop(0,seqs,chunk2,0)

    pltpu.make_async_copy(normed_t,a_t.at[:,pl.ds(0,seq)],at_sem).wait()
    for c in range(seqs):
        from_all(h_seq,h_send.at[c],h_recv.at[c]).wait_send()
        from_all(do_seq,d_send.at[c],d_recv.at[c]).wait_send()
    from_all(tab_all,t_send,t_recv).wait_send()

def exchange_call(hidden,d_out,tab,gain,w_qkv,w_out):
    n,loc,dim=hidden.shape
    group=16
    rows=n*loc
    seqs=n//group; seq=loc*group
    any_=pl.BlockSpec(memory_space=pl.ANY)
    D=pltpu.SemaphoreType.DMA
    S=jax.ShapeDtypeStruct
    return pl.pallas_call(
        exchange_kernel,
        in_specs=[any_,any_,any_,pl.BlockSpec(memory_space=pltpu.VMEM),any_,any_],
        out_specs=[any_]*6,
        out_shape=[S((rows,dim),BF),S((rows,dim),BF),S((seq,256),F32),S((dim,rows),BF),S((3,rows,dim),BF),S((rows,dim),BF)],
        scratch_shapes=[pltpu.VMEM((2*seqs,loc,dim),BF),pltpu.VMEM((loc,256),F32),pltpu.VMEM((seq,dim),BF),pltpu.VMEM((seq,dim),BF),pltpu.VMEM((dim,seq),BF),pltpu.VMEM((seq,256),F32),
            D((seqs,)),D((seqs,)),D((seqs,)),D((seqs,)),D,D,D((2*seqs+1,)),D,D],
        compiler_params=pltpu.CompilerParams(collective_id=0,has_side_effects=True,vmem_limit_bytes=48<<20),
        cost_estimate=pl.CostEstimate(flops=8*rows*dim*dim,bytes_accessed=40*dim*dim,transcendentals=0),
        name="exchange",
    )(hidden,d_out,tab,gain,w_qkv,w_out)


TW = 256
PARTS = ((0, 384), (384, 320), (704, 320))
NS = 3
NB = 7
BLK = 256


def attend(scale, qkv, do, tabs, o_out, o_t_out, dproj_out):
    seq = qkv.shape[1]
    for h in range(2):
        cols = slice(h * 128, (h + 1) * 128)
        q = qkv[0, :, cols]
        k = qkv[1, :, cols]
        v = qkv[2, :, cols]
        dout = do[:, cols]
        k_t = k.T
        v_t = v.T
        dk = [None] * (seq // BLK)
        dv = [None] * (seq // BLK)
        for j in range(seq // BLK):
            end = (j + 1) * BLK
            rows = slice(j * BLK, end)
            q_j = q[rows]
            do_j = dout[rows]
            s = dot_nt(k[:end], q_j)
            row = lax.broadcasted_iota(jnp.int32, (end, BLK), 0)
            col = lax.broadcasted_iota(jnp.int32, (end, BLK), 1) + j * BLK
            s = jnp.where(row <= col, s * scale, -1e30)
            m = jnp.max(s, axis=0, keepdims=True)
            e = jnp.exp(s - m)
            p = e * (1.0 / jnp.sum(e, axis=0, keepdims=True))
            p_bf = p.astype(BF)
            o_t = dot_nn(v_t[:, :end], p_bf)
            dp = dot_nt(v[:end], do_j).astype(BF).astype(F32)
            delta = jnp.sum(p * dp, axis=0, keepdims=True)
            ds = (p * (dp - delta) * scale).astype(BF)
            dv_j = dot_nn(p_bf, do_j)
            dk_j = dot_nn(ds, q_j)
            dq_t = dot_nn(k_t[:, :end], ds)
            for i in range(j + 1):
                part = slice(i * BLK, (i + 1) * BLK)
                dv[i] = dv_j[part] if dv[i] is None else dv[i] + dv_j[part]
                dk[i] = dk_j[part] if dk[i] is None else dk[i] + dk_j[part]
            o_out[rows, cols] = o_t.T.astype(BF)
            o_t_out[cols, rows] = o_t.astype(BF)
            dq = dq_t.T.astype(BF).astype(F32)
            dproj_out[0, rows, cols] = unrotate(dq, tabs[rows, :128], tabs[rows, 128:]).astype(BF)
        for j in range(seq // BLK):
            rows = slice(j * BLK, (j + 1) * BLK)
            dkj = dk[j].astype(BF).astype(F32)
            dproj_out[1, rows, cols] = unrotate(dkj, tabs[rows, :128], tabs[rows, 128:]).astype(BF)
            dproj_out[2, rows, cols] = dv[j].astype(BF)


def main_kernel(scale, a_t, qkv, d_attn, tab_all, h_seq, do_seq, w_qkv, w_out, gain_ref,
                g_hbm, o_hbm, o_t_hbm, dproj_hbm, y_hbm, dh_hbm, dgain_ref,
                lhs, dproj_v, acc, r0, r1, r2, r3, qkv_v, do_v, o_v, o_t_v, tabs, o_chunk, dn_acc, h_v, dout_v, dh_v, dg_all,
                lhs_sem, ld_sem, s_send, s_recv, credit, loc_sem, g_send, g_recv,
                in_sem, out_sem, rhs_sem, dh_sem, dg_send, dg_recv):
    me = lax.axis_index('sp')
    group = 16
    dim, rows_all = a_t.shape
    seq = tab_all.shape[0]
    seqs = rows_all // seq
    loc = seq // group
    half = dim // 2
    n_qkv = 3 * dim // TW
    n_all = 4 * dim // TW
    pairs = dim // TW
    core = me % 2
    mate = me + 1 - 2 * core
    recv = (r0, r1, r2, r3)

    def remote(src, dst, ss, rs, peer):
        return pltpu.make_async_remote_copy(src_ref=src, dst_ref=dst, send_sem=ss, recv_sem=rs, device_id=(peer,), device_id_type=MESH)

    def link(d):
        w = 2 + d + d * d
        bit = (me // w) % 2
        return bit, me + w * (1 - 2 * bit)

    def aligned(x, n):
        return pl.multiple_of(x, n)

    def dims(u, p, t):
        return (u + p + t - 1) % 3

    def offs(u, p, size):
        o = [0]
        for t in (1, 2, 3):
            b, _ = link(dims(u, p, t))
            o.append(o[-1] + b * (size >> t))
        return o

    def rs_all(u, t):
        sl = u % NS
        return remote(recv[t].at[sl], recv[t].at[sl], s_send.at[t, sl], s_recv.at[t, sl], mate)

    def rs_start(u, t):
        sl, nb = u % NS, u % NB

        @pl.when(u >= NS)
        def _():
            pl.semaphore_wait(credit.at[t, sl], 1 if t == 0 else 3)
            rs_all(u, t).wait_send()

        if t == 0:
            src = acc.at[nb, pl.ds(aligned((1 - core) * half, half), half)]
            remote(src, r0.at[sl], s_send.at[0, sl], s_recv.at[0, sl], mate).start()
            return
        for p, (base, size) in enumerate(PARTS):
            o = offs(u, p, size)
            n = size >> t
            b, peer = link(dims(u, p, t))
            row = core * half + base + o[t - 1] + (1 - b) * n
            remote(acc.at[nb, pl.ds(aligned(row, 8), n)], recv[t].at[sl, pl.ds(base >> t, n)],
                   s_send.at[t, sl], s_recv.at[t, sl], peer).start()

    def rs_finish(u, t):
        sl, nb = u % NS, u % NB
        rs_all(u, t).wait_recv()
        if t == 0:
            rows = pl.ds(aligned(core * half, half), half)
            acc[nb, rows] = acc[nb, rows] + r0[sl]
            pl.semaphore_signal(credit.at[0, sl], inc=1, device_id=(mate,), device_id_type=MESH)
            return
        for p, (base, size) in enumerate(PARTS):
            n = size >> t
            rows = pl.ds(aligned(core * half + base + offs(u, p, size)[t], 8), n)
            acc[nb, rows] = acc[nb, rows] + recv[t][sl, pl.ds(base >> t, n)]
            pl.semaphore_signal(credit.at[t, sl], inc=1, device_id=(link(dims(u, p, t))[1],), device_id_type=MESH)

    def tile_col(u):
        return jnp.where(u < n_qkv, (u % 3) * pairs + u // 3, u) * TW

    def g_at(u, row, n):
        return g_hbm.at[pl.ds(aligned(row, 8), n), pl.ds(aligned(tile_col(u), TW), TW)]

    def ag_all(u, t):
        r = g_hbm.at[pl.ds(0, half >> t), pl.ds(0, TW)]
        return remote(r, r, g_send.at[t, u % NS], g_recv.at[t, u], mate)

    def ag_start(u, t):
        @pl.when(u >= NS)
        def _():
            ag_all(u, t).wait_send()

        if t == 0:
            r = g_at(u, core * half, half)
            remote(r, r, g_send.at[0, u % NS], g_recv.at[0, u], mate).start()
            return
        for p, (base, size) in enumerate(PARTS):
            n = size >> t
            row = core * half + base + offs(u, p, size)[t]
            dst = g_at(u, row, n)
            src = acc.at[u % NB, pl.ds(aligned(row, 8), n)] if t == 3 else dst
            remote(src, dst, g_send.at[t, u % NS], g_recv.at[t, u], link(dims(u, p, t))[1]).start()

    def local_start(u):
        for p, (base, size) in enumerate(PARTS):
            n = size >> 3
            row = core * half + base + offs(u, p, size)[3]
            pltpu.make_async_copy(acc.at[u % NB, pl.ds(aligned(row, 8), n)], g_at(u, row, n), loc_sem.at[u % NS]).start()

    def local_wait(u):
        n = half >> 3
        pltpu.make_async_copy(acc.at[0, pl.ds(0, n)], g_hbm.at[pl.ds(0, n), pl.ds(0, TW)], loc_sem.at[u % NS]).wait()

    def attn_in(a):
        s, p, sl = a % seqs, a // seqs, a % 2
        rows = pl.ds(aligned(s * seq, seq), seq)
        cols = pl.ds(aligned(p * TW, TW), TW)
        return (pltpu.make_async_copy(qkv.at[:, rows, cols], qkv_v.at[sl], in_sem.at[0, sl]),
                pltpu.make_async_copy(d_attn.at[rows, cols], do_v.at[sl], in_sem.at[1, sl]))

    def attn_out(a):
        s, p, sl = a % seqs, a // seqs, a % 2
        rows = pl.ds(aligned(s * seq, seq), seq)
        cols = pl.ds(aligned(p * TW, TW), TW)
        return (pltpu.make_async_copy(o_v.at[sl], o_hbm.at[rows, cols], out_sem.at[0, sl]),
                pltpu.make_async_copy(o_t_v.at[sl], o_t_hbm.at[cols, rows], out_sem.at[1, sl]),
                pltpu.make_async_copy(dproj_v.at[p % 2, :, rows], dproj_hbm.at[:, rows, cols], out_sem.at[2, sl]))

    n_attn = seqs * pairs

    def attn_step(a):
        @pl.when(a + 1 < n_attn)
        def _():
            for c in attn_in(a + 1):
                c.start()

        for c in attn_in(a):
            c.wait()

        @pl.when(a >= 2)
        def _():
            for c in attn_out(a - 2):
                c.wait()

        s, p, sl = a % seqs, a // seqs, a % 2
        attend(scale, qkv_v.at[sl], do_v.at[sl], tabs, o_v.at[sl], o_t_v.at[sl], dproj_v.at[p % 2, :, pl.ds(aligned(s * seq, seq), seq)])
        for c in attn_out(a):
            c.start()

    def rhs_copy(u):
        j = u - n_qkv
        return pltpu.make_async_copy(do_seq.at[:, pl.ds(aligned(j * TW, TW), TW)], dproj_v.at[0, j % 3], rhs_sem.at[j % 3])

    def dw_tile(u):
        @pl.when(u == n_qkv)
        def _():
            pltpu.make_async_copy(o_t_hbm, lhs, lhs_sem).wait()

        @pl.when(u >= n_qkv)
        def _():
            rhs_copy(u).wait()

        p = jnp.where(u < n_qkv, (u // 3) % 2, 0)

        @pl.loop(0, dim // 512)
        def _(b):
            rows = pl.ds(aligned(b * 512, 512), 512)
            acc[u % NB, rows] = dot_nn(lhs[rows], dproj_v[p, u % 3])

        rs_start(u, 0)

        @pl.when(u == n_qkv - 1)
        def _():
            pltpu.make_async_copy(o_t_hbm, lhs, lhs_sem).start()

        @pl.when(jnp.logical_and(u + 2 >= n_qkv, u + 2 < n_all))
        def _():
            rhs_copy(u + 2).start()

    def seq_rows(c):
        return pl.ds(aligned(c * seq, seq), seq)

    def out_proj(c):
        def body(o_ref, w_ref, h_ref, y_ref):
            y = h_ref[...].astype(F32) + dot_nn(o_ref[...], w_ref[...])
            y_ref[...] = y.astype(BF).reshape(group, loc, y.shape[1])

        tn = 512
        pltpu.emit_pipeline(
            body, grid=(dim // tn,),
            in_specs=[pl.BlockSpec((seq, dim), lambda n: (0, 0)), pl.BlockSpec((dim, tn), lambda n: (0, n)), pl.BlockSpec((seq, tn), lambda n: (0, n))],
            out_specs=[pl.BlockSpec((group, loc, tn), lambda n: (0, 0, n))],
        )(o_hbm.at[seq_rows(c)], w_out, h_seq.at[seq_rows(c)], y_hbm.at[:, c])

    TK = 512
    per = dim // TK

    def d_normed(c, third):
        @pl.when(third == 0)
        def _():
            pltpu.make_async_copy(h_seq.at[seq_rows(c)], h_v, dh_sem.at[0]).start()
            pltpu.make_async_copy(do_seq.at[seq_rows(c)], dout_v, dh_sem.at[1]).start()

        def body(p_ref, w_ref):
            part = dot_nt(p_ref[...], w_ref[...])
            first = jnp.logical_and(third == 0, pl.program_id(0) == 0)

            @pl.when(first)
            def _():
                dn_acc[...] = part

            @pl.when(jnp.logical_not(first))
            def _():
                dn_acc[...] += part

        pltpu.emit_pipeline(
            body, grid=(per,),
            in_specs=[pl.BlockSpec((seq, TK), lambda n: (0, n)), pl.BlockSpec((dim, TK), lambda n: (0, n))],
        )(dproj_hbm.at[third, seq_rows(c)], w_qkv.at[:, pl.ds(aligned(third * dim, dim), dim)])

        @pl.when(third == 2)
        def _():
            pltpu.make_async_copy(h_seq.at[seq_rows(c)], h_v, dh_sem.at[0]).wait()
            pltpu.make_async_copy(do_seq.at[seq_rows(c)], dout_v, dh_sem.at[1]).wait()

            @pl.when(c > 0)
            def _():
                pltpu.make_async_copy(dh_v, dh_hbm.at[:, c], dh_sem.at[2]).wait()

            gain = gain_ref[...].astype(F32)

            @pl.loop(0, group)
            def _(b):
                r = pl.ds(aligned(b * loc, loc), loc)
                h = h_v[r].astype(F32)
                inv = lax.rsqrt(jnp.mean(h * h, axis=-1, keepdims=True) + NORM_EPS)
                dn = dn_acc[r].astype(BF).astype(F32)
                dg = jnp.sum(dn * h * inv, axis=0, keepdims=True)
                ds = dn * gain
                dh = dout_v[r].astype(F32) + inv * ds - h * (inv * inv * inv) * jnp.mean(ds * h, axis=-1, keepdims=True)
                dh_v[b] = dh.astype(BF)
                first = jnp.logical_and(c == 0, b == 0)

                @pl.when(first)
                def _():
                    dg_all[me] = dg

                @pl.when(jnp.logical_not(first))
                def _():
                    dg_all[me] += dg

            pltpu.make_async_copy(dh_v, dh_hbm.at[:, c], dh_sem.at[2]).start()

    barrier = pltpu.get_barrier_semaphore()
    for j in range(1, group):
        pl.semaphore_signal(barrier, inc=1, device_id=(flipped(me, j),), device_id_type=MESH)
    for c in attn_in(0):
        c.start()
    pltpu.make_async_copy(a_t, lhs, lhs_sem).start()
    pltpu.make_async_copy(tab_all, tabs, ld_sem).start()
    pltpu.make_async_copy(tab_all, tabs, ld_sem).wait()
    pl.loop(0, seqs)(attn_step)
    pltpu.make_async_copy(a_t, lhs, lhs_sem).wait()
    pl.semaphore_wait(barrier, group - 1)

    first_out = 3 * (pairs - 1)
    first_dn = first_out + seqs

    def step(i, carry):
        def guarded(lag, fn):
            u = i - lag

            @pl.when(jnp.logical_and(u >= 0, u < n_all))
            def _():
                fn(u)

        def ag0(u):
            ag_all(u, 0).wait_recv()

        def ag1(u):
            ag_all(u, 1).wait_recv()
            ag_start(u, 0)

        def ag2(u):
            ag_all(u, 2).wait_recv()
            ag_start(u, 1)

        def ag3(u):
            ag_all(u, 3).wait_recv()
            local_wait(u)
            ag_start(u, 2)

        def last(u):
            rs_finish(u, 3)
            local_start(u)
            ag_start(u, 3)

        def middle(t):
            def fn(u):
                rs_finish(u, t)
                rs_start(u, t + 1)
            return fn

        for lag, fn in ((1, middle(0)), (2, middle(1)), (3, middle(2)), (4, last), (5, ag3), (6, ag2), (7, ag1), (8, ag0), (0, dw_tile)):
            guarded(lag, fn)

        p, r = i // 3 + 1, i % 3

        @pl.when(p < pairs)
        def _():
            lo = (4 * r + 2) // 3
            hi = (4 * r + 6) // 3

            @pl.loop(lo, hi)
            def _(s):
                attn_step(p * seqs + s)

        @pl.when(i == first_out)
        def _():
            for c in attn_out(n_attn - 2) + attn_out(n_attn - 1):
                c.wait()

        @pl.when(jnp.logical_and(i >= first_out, i < first_dn))
        def _():
            out_proj(i - first_out)

        @pl.when(jnp.logical_and(i >= first_dn, i < first_dn + 3 * seqs))
        def _():
            d_normed((i - first_dn) // 3, (i - first_dn) % 3)

        @pl.when(i == first_dn + 3 * seqs)
        def _():
            for j in range(1, group):
                remote(dg_all.at[me], dg_all.at[me], dg_send, dg_recv, flipped(me, j)).start()

        return carry

    lax.fori_loop(0, n_all + 8, step, 0)

    pltpu.make_async_copy(dh_v, dh_hbm.at[:, 0], dh_sem.at[2]).wait()
    others = remote(dg_all.at[pl.ds(0, group - 1)], dg_all.at[pl.ds(0, group - 1)], dg_send, dg_recv, mate)
    others.wait_recv()
    others.wait_send()
    dgain = dg_all[0]
    for j in range(1, group):
        dgain = dgain + dg_all[j]
    dgain_ref[...] = dgain
    for j in range(NS):
        u = n_all - NS + j
        for t in range(4):
            rs_all(u, t).wait_send()
            pl.semaphore_wait(credit.at[t, u % NS], 1 if t == 0 else 3)
            ag_all(u, t).wait_send()


def main_call(a_t, qkv, d_attn, tab, h_seq, do_seq, w_qkv, w_out, gain):
    dim, rows = a_t.shape
    seq = tab.shape[0]
    seqs = rows // seq
    group = 16
    loc = seq // group
    h = dim // 2
    n_all = 4 * dim // TW
    hbm = pl.BlockSpec(memory_space=pl.ANY)
    vmem = pl.BlockSpec(memory_space=pltpu.VMEM)
    D = pltpu.SemaphoreType.DMA
    S = jax.ShapeDtypeStruct
    V = pltpu.VMEM
    return pl.pallas_call(
        functools.partial(main_kernel, 128 ** -0.5),
        in_specs=[hbm] * 8 + [vmem],
        out_specs=[hbm] * 6 + [vmem],
        out_shape=[S((dim, 4 * dim), F32), S((rows, dim), BF), S((dim, rows), BF), S((3, rows, dim), BF),
                   S((group, seqs, loc, dim), BF), S((group, seqs, loc, dim), BF), S((1, dim), F32)],
        scratch_shapes=[
            V((dim, rows), BF), V((2, 3, rows, TW), BF), V((NB, dim, TW), F32),
            V((NS, h, TW), F32), V((NS, h >> 1, TW), F32), V((NS, h >> 2, TW), F32), V((NS, h >> 3, TW), F32),
            V((2, 3, seq, TW), BF), V((2, seq, TW), BF), V((2, seq, TW), BF), V((2, TW, seq), BF), V((seq, 256), F32),
            V((8, 128), BF), V((seq, dim), F32), V((seq, dim), BF), V((seq, dim), BF), V((group, loc, dim), BF), V((group, 1, dim), F32),
            D, D, D((4, NS)), D((4, NS)), pltpu.SemaphoreType.REGULAR((4, NS)), D((NS,)), D((4, NS)), D((4, n_all)),
            D((2, 2)), D((3, 2)), D((3,)), D((3,)), D, D,
        ],
        compiler_params=pltpu.CompilerParams(collective_id=1, has_side_effects=True, vmem_limit_bytes=67043328),
        cost_estimate=pl.CostEstimate(flops=20 * rows * dim * dim, bytes_accessed=60 * dim * dim, transcendentals=0),
        name="main",
    )(a_t, qkv, d_attn, tab, h_seq, do_seq, w_qkv, w_out, gain)


def solution(mesh):
    group = mesh.shape['sp']
    token_spec = P(None, 'sp', None)
    table_spec = P('sp', None)

    def device_step(hidden, norm_gain, w_qkv, w_out, cos_tab, sin_tab, d_out):
        num_seqs, local_len, dim = hidden.shape
        mine = num_seqs // group
        seq = local_len * group
        rows = mine * seq

        def to_tokens(x):
            x = lax.all_to_all(x, 'sp', split_axis=0, concat_axis=0, tiled=True)
            return x.reshape(num_seqs, local_len, dim)

        gain = norm_gain.reshape(1, dim)
        tab = jnp.concatenate([cos_tab, cos_tab, -sin_tab, sin_tab], axis=1)
        h_seq, do_seq, tab, normed_t, qkv, d_attn = exchange_call(hidden, d_out, tab, gain, w_qkv, w_out)
        dw, _, _, _, y, dh, dgain = main_call(normed_t, qkv, d_attn, tab, h_seq, do_seq, w_qkv, w_out, gain)
        y = to_tokens(y)
        dh = to_tokens(dh)
        return y, dh, dw[:, :3 * dim], dw[:, 3 * dim:], dgain.reshape(dim)

    return jax.shard_map(device_step, mesh=mesh, in_specs=(token_spec, P(None), P(None, None), P(None, None), table_spec, table_spec, token_spec), out_specs=(token_spec, token_spec, P(None, None), P(None, None), P(None)), check_vma=False)
```

time: 2170 us -> 947 us (0.44)
  waiting for transfers between devices: 905 us -> 60.6 us
  Pallas kernels: 0 us -> 712 us
  matrix products: 560 us -> 0 us
  local copies, waits for them, and re-layouts: 404 us -> 65.3 us
  other arithmetic: 201 us -> 1.59 us
  blocking collectives: 34.1 us -> 97.9 us
  starting transfers between devices: 34.8 us -> 4.63 us
    pallas_call x0 -> x2, Pallas kernels: none -> 712 us  [the longest x1 507 us: main_call(): pl.pallas_call(functools.partial(main_kernel, 128 ** (-0.5)), in_specs=[h...]
    dot_general x11 -> x0, matrix products: 527 us -> none  [the longest x1 85.9 us: device_step(): jnp.einsum('bhqk,bqhd->bkhd', d_scores, q_heads, preferred_element_type=j...]
    psum x1 -> x0, waiting for transfers between devices: 445 us -> none  [device_step(): lax.psum(jnp.einsum('btd,bte->de', normed, d_proj, preferred_element_type...]
    all_to_all x8 -> x1, waiting for transfers between devices: 460 us -> 60.6 us  [to_tokens(): x = lax.all_to_all(x, 'sp', split_axis=0, concat_axis=0, tiled=True)]
    all_to_all x9 -> x0, local copies, waits for them, and re-layouts: 101 us -> none  [the longest x2 27.4 us: device_step(): attn_local = to_tokens(attn_heads).reshape(num_seqs, local_len, model_dim)]
    all_to_all x0 -> x1, blocking collectives: none -> 97.9 us  [to_tokens(): x = lax.all_to_all(x, 'sp', split_axis=0, concat_axis=0, tiled=True)]
    convert_element_type x4 -> x0, other arithmetic: 91.6 us -> none  [the longest x1 42.1 us: device_step(): (projected[:, :, 1] * cos_full + rotate_half(projected[:, :, 1]) * sin_fu...]
    unnamed x30 -> x9, local copies, waits for them, and re-layouts: 98.5 us -> 18.3 us
  transfers between devices with their start and end apart: 9 -> 1, of which waited for: 8 -> 1; matrix products, arithmetic and copies ran while one was open for 26% -> 5% of each run, Pallas kernels for 0% -> 0%
where the time goes in v2:
time: 947 us; the launch traced here: 943 us
  Pallas kernels  712 us (75%)
  blocking collectives  97.9 us (10%)
  local copies, waits for them, and re-layouts  65.3 us (7%)
  waiting for transfers between devices  60.6 us (6%)
    pallas_call x1, Pallas kernels, main_call(): pl.pallas_call(functools.partial(main_kernel, 128 ** (-0.5)), in_specs=[h...  507 us
    pallas_call x1, Pallas kernels, exchange_call(): pl.pallas_call(exchange_kernel, in_specs=[any_, any_, any_, pl.BlockSpec(...  205 us
    all_to_all x1, blocking collectives, to_tokens(): x = lax.all_to_all(x, 'sp', split_axis=0, concat_axis=0, tiled=True)  97.9 us
    all_to_all x1, waiting for transfers between devices, to_tokens(): x = lax.all_to_all(x, 'sp', split_axis=0, concat_axis=0, tiled=True)  60.6 us
    slice x2, local copies, waits for them, and re-layouts, device_step(): return (y, dh, dw[:, :3 * dim], dw[:, 3 * dim:], dgain.reshape(dim))  46.3 us
  transfers between devices with their start and end apart: 1, of which 1 were waited for; matrix products, arithmetic and copies ran while one was open for 5% of the time, Pallas kernels for 0%

profile of v2, /device:TPU:0, one launch (start us, length us, event | category | flops | bytes accessed | tf_op | source)
XLA Modules:
  0.0 942.9 jit_solution(1845768977230074249)
XLA Ops:
  0.6 0.7 reshape.22.gain_ref
  1.3 0.0 copy-start
  1.3 0.7 neg.3
  2.1 0.9 pad_maximum_fusion.tab
  2.9 205.2 %exchange.1 = (bf16[2048,2048]{1,0:T(8,128)(2,1)}, bf16[2048,2048]{1,0:T(8,128)(2,1)}, f32[512,256]{1,0:T(8,128)S(1)}, bf16[2048,2048]{1,0:T(8,128)(2,1)}, bf16[...) custom-call(bf16[64,32,2048]{2,1,0:T(8,128)(2,1)} %hidden.1, bf16[64,32,2048]{2,1,0:T(8,128)(2,1)} %d_out.1, ...), custom_call_target="tpu_custom_call" | custom-call | flops 68719476736 | bytes 167772160 | tf_op jit(solution)/shard_map/exchange/pallas_call | solution.py:152
  208.1 0.0 copy-done
  208.1 0.0 copy-start.1
  208.2 0.8 copy-done.1
  208.9 506.9 %main.1 = (f32[2048,8192]{1,0:T(8,128)}, bf16[2048,2048]{1,0:T(8,128)(2,1)}, bf16[2048,2048]{1,0:T(8,128)(2,1)}, bf16[3,2048,2048]{2,1,0:T(8,128)(2,1)}, bf16[16...) custom-call(bf16[2048,2048]{1,0:T(8,128)(2,1)} %get-tuple-element.15.a_t, ...), custom_call_target="tpu_custom_call" | custom-call | flops 171798691840 | bytes 251658240 | tf_op jit(solution)/shard_map/main/pallas_call | solution.py:588
  715.8 97.9 %all_to_all.10 = bf16[16,4,32,2048]{3,2,1,0:T(8,128)(2,1)} all-to-all(bf16[16,4,32,2048]{3,2,1,0:T(8,128)(2,1)} %get-tuple-element.21), channel_id=1, replica_groups=mesh['sp'=16] {'sp'}, dimensions={0} | all-to-all | bytes 16777216 | tf_op jit(solution)/shard_map/all_to_all | solution.py:620
  813.8 4.6 all-to-all-start.1
  818.4 11.8 %slice.7 = f32[2048,2048]{1,0:T(8,128)} slice(f32[2048,8192]{1,0:T(8,128)} %get-tuple-element.23), slice={[0:2048], [6144:8192]} | slice | bytes 33554432 | tf_op jit(solution)/shard_map/slice | solution.py:629
  830.2 34.5 %slice.6 = f32[2048,6144]{1,0:T(8,128)} slice(f32[2048,8192]{1,0:T(8,128)} %get-tuple-element.23), slice={[0:2048], [0:6144]} | slice | bytes 100663296 | tf_op jit(solution)/shard_map/slice | solution.py:629
  864.7 60.6 %all-to-all-done.1 = bf16[16,4,32,2048]{3,2,1,0:T(8,128)(2,1)} async-done(((bf16[16,4,32,2048]{3,2,1,0:T(8,128)(2,1)}), bf16[16,4,32,2048]{3,2,1,0:T(8,128)(2,1)}, u32[]{:S(2)}, u32[]{:S(2)}) %all-to-all-start.1) | async-done | bytes 8388640 | tf_op jit(solution)/shard_map/all_to_all | solution.py:620
  925.4 8.4 copy.15
  933.8 0.0 copy-start.2
  933.8 8.5 copy.16
  942.2 0.0 copy-done.2
  942.3 0.6 copy.17
Async XLA Ops:
  1.3 206.8 %copy-start = (bf16[1,2048]{1,0:T(2,128)(2,1)}, bf16[1,2048]{1,0:T(2,128)(2,1)S(1)}, u32[]{:S(2)}) copy-start(bf16[1,2048]{1,0:T(2,128)(2,1)S(1)} %reshape.22.gain_ref) | copy-start | bytes 12292
  208.1 0.8 copy-start.1
  813.8 111.6 %all-to-all-start.1 = ((bf16[16,4,32,2048]{3,2,1,0:T(8,128)(2,1)}), bf16[16,4,32,2048]{3,2,1,0:T(8,128)(2,1)}, u32[]{:S(2)}, u32[]{:S(2)}) async-start(bf16[16,4,32,2048]{3,2,1,0:T(8,128)(2,1)} %get-tuple-element.22), calls=%async_computation.1 | async-start | bytes 16777216 | tf_op jit(solution)/shard_map/all_to_all | solution.py:620
  933.8 8.5 copy-start.2

commit v3 on v2

v3 whole, which is shorter than its diff:
```python
import functools
import jax
import jax.numpy as jnp
from jax import lax
from jax.experimental import pallas as pl
from jax.experimental.pallas import tpu as pltpu
from jax.sharding import PartitionSpec as P

NORM_EPS = 1e-6
BF = jnp.bfloat16
F32 = jnp.float32
VMEM_LIMIT = 60 * 1024 * 1024


def dot_nn(a, b):
    return lax.dot_general(a, b, (((1,), (0,)), ((), ())), preferred_element_type=F32)


def dot_nt(a, b):
    return lax.dot_general(a, b, (((1,), (1,)), ((), ())), preferred_element_type=F32)


def rotate(u, cos, sin_signed):
    return u * cos + pltpu.roll(u, 64, 1) * sin_signed


def unrotate(u, cos, sin_signed):
    return u * cos - pltpu.roll(u, 64, 1) * sin_signed


MESH = pl.DeviceIdType.MESH


def flipped(me, j):
    p = me
    for b in range(4):
        w = 1 << b
        if j & w:
            p = p + w * (1 - 2 * ((me // w) % 2))
    return p


ORDER = tuple(int(j, 16) for j in '2481359' + '6ac7bdef')


TW = 256
PARTS = ((0, 384), (384, 320), (704, 320))
NS = 3
NB = 6
BLK = 256


def attend(scale, qkv, do, tabs, o_out, o_t_out, dproj_out):
    seq = qkv.shape[1]
    for h in range(2):
        cols = slice(h * 128, (h + 1) * 128)
        q = qkv[0, :, cols]
        k = qkv[1, :, cols]
        v = qkv[2, :, cols]
        dout = do[:, cols]
        k_t = k.T
        v_t = v.T
        dk = [None] * (seq // BLK)
        dv = [None] * (seq // BLK)
        for j in range(seq // BLK):
            end = (j + 1) * BLK
            rows = slice(j * BLK, end)
            q_j = q[rows]
            do_j = dout[rows]
            s = dot_nt(k[:end], q_j)
            row = lax.broadcasted_iota(jnp.int32, (end, BLK), 0)
            col = lax.broadcasted_iota(jnp.int32, (end, BLK), 1) + j * BLK
            s = jnp.where(row <= col, s * scale, -1e30)
            m = jnp.max(s, axis=0, keepdims=True)
            e = jnp.exp(s - m)
            p = e * (1.0 / jnp.sum(e, axis=0, keepdims=True))
            p_bf = p.astype(BF)
            o_t = dot_nn(v_t[:, :end], p_bf)
            dp = dot_nt(v[:end], do_j).astype(BF).astype(F32)
            delta = jnp.sum(p * dp, axis=0, keepdims=True)
            ds = (p * (dp - delta) * scale).astype(BF)
            dv_j = dot_nn(p_bf, do_j)
            dk_j = dot_nn(ds, q_j)
            dq_t = dot_nn(k_t[:, :end], ds)
            for i in range(j + 1):
                part = slice(i * BLK, (i + 1) * BLK)
                dv[i] = dv_j[part] if dv[i] is None else dv[i] + dv_j[part]
                dk[i] = dk_j[part] if dk[i] is None else dk[i] + dk_j[part]
            o_out[rows, cols] = o_t.T.astype(BF)
            o_t_out[cols, rows] = o_t.astype(BF)
            dq = dq_t.T.astype(BF).astype(F32)
            dproj_out[0, rows, cols] = unrotate(dq, tabs[rows, :128], tabs[rows, 128:]).astype(BF)
        for j in range(seq // BLK):
            rows = slice(j * BLK, (j + 1) * BLK)
            dkj = dk[j].astype(BF).astype(F32)
            dproj_out[1, rows, cols] = unrotate(dkj, tabs[rows, :128], tabs[rows, 128:]).astype(BF)
            dproj_out[2, rows, cols] = dv[j].astype(BF)


def main_kernel(scale, hidden, d_out, cos_ref, sin_ref, w_qkv, w_out, gain_ref,
                g_hbm, h_seq, do_seq, qkv, o_hbm, o_t_hbm, dproj_hbm, y_all, dh_hbm, dh_loc, dh_all, dgain_ref,
                lhs, dproj_v, acc, r0, r1, r2, r3, qkv_v, do_v, o_v, o_t_v, tabs, tab, dn_acc, h_v, dout_v, dh_v, dg_all, wbuf, pbuf, o_c, y_t,
                lhs_sem, ld_sem, s_send, s_recv, credit, loc_sem, g_send, g_recv,
                in_sem, out_sem, rhs_sem, dh_sem, dg_send, dg_recv, w_sem, o_sem, c0_sem,
                h_send, h_recv, d_send, d_recv, t_send, t_recv, own_sem, y_send, y_recv, y_own, x_send, x_recv):
    me = lax.axis_index('sp')
    group = 16
    loc, dim = hidden.shape[1:]
    seqs = hidden.shape[0] // group
    seq = loc * group
    half = dim // 2
    n_qkv = 3 * dim // TW
    n_all = 4 * dim // TW
    pairs = dim // TW
    core = me % 2
    mate = me + 1 - 2 * core
    recv = (r0, r1, r2, r3)
    TN = 512
    per = dim // TN

    def remote(src, dst, ss, rs, peer):
        return pltpu.make_async_remote_copy(src_ref=src, dst_ref=dst, send_sem=ss, recv_sem=rs, device_id=(peer,), device_id_type=MESH)

    def link(d):
        w = 2 + d + d * d
        bit = (me // w) % 2
        return bit, me + w * (1 - 2 * bit)

    def aligned(x, n):
        return pl.multiple_of(x, n)

    def dims(u, p, t):
        return (u + p + t - 1) % 3

    def offs(u, p, size):
        o = [0]
        for t in (1, 2, 3):
            b, _ = link(dims(u, p, t))
            o.append(o[-1] + b * (size >> t))
        return o

    def rs_all(u, t):
        sl = u % NS
        return remote(recv[t].at[sl], recv[t].at[sl], s_send.at[t, sl], s_recv.at[t, sl], mate)

    def rs_start(u, t):
        sl, nb = u % NS, u % NB

        @pl.when(u >= NS)
        def _():
            pl.semaphore_wait(credit.at[t, sl], 1 if t == 0 else 3)

        if t == 0:
            n = half // 4
            for k in range(4):
                src = acc.at[nb, pl.ds(aligned((1 - core) * half + k * n, n), n)]
                remote(src, r0.at[sl, pl.ds(k * n, n)], s_send.at[0, sl], s_recv.at[0, sl], mate).start()
            return
        for p, (base, size) in enumerate(PARTS):
            o = offs(u, p, size)
            n = size >> t
            b, peer = link(dims(u, p, t))
            row = core * half + base + o[t - 1] + (1 - b) * n
            remote(acc.at[nb, pl.ds(aligned(row, 8), n)], recv[t].at[sl, pl.ds(base >> t, n)],
                   s_send.at[t, sl], s_recv.at[t, sl], peer).start()

    def rs_finish(u, t):
        sl, nb = u % NS, u % NB
        rs_all(u, t).wait_recv()
        rs_all(u, t).wait_send()
        if t == 0:
            rows = pl.ds(aligned(core * half, half), half)
            acc[nb, rows] = acc[nb, rows] + r0[sl]
            pl.semaphore_signal(credit.at[0, sl], inc=1, device_id=(mate,), device_id_type=MESH)
            return
        for p, (base, size) in enumerate(PARTS):
            n = size >> t
            rows = pl.ds(aligned(core * half + base + offs(u, p, size)[t], 8), n)
            acc[nb, rows] = acc[nb, rows] + recv[t][sl, pl.ds(base >> t, n)]
            pl.semaphore_signal(credit.at[t, sl], inc=1, device_id=(link(dims(u, p, t))[1],), device_id_type=MESH)

    def tile_col(u):
        return jnp.where(u < n_qkv, (u % 3) * pairs + u // 3, u) * TW

    def g_at(u, row, n):
        return g_hbm.at[pl.ds(aligned(row, 8), n), pl.ds(aligned(tile_col(u), TW), TW)]

    def ag_all(u, t):
        r = g_hbm.at[pl.ds(0, half >> t), pl.ds(0, TW)]
        return remote(r, r, g_send.at[t, u % NS], g_recv.at[t, u], mate)

    def ag_start(u, t):
        if t < 3:
            @pl.when(u >= NS)
            def _():
                ag_all(u, t).wait_send()

        if t == 0:
            r = g_at(u, core * half, half)
            remote(r, r, g_send.at[0, u % NS], g_recv.at[0, u], mate).start()
            return
        for p, (base, size) in enumerate(PARTS):
            n = size >> t
            row = core * half + base + offs(u, p, size)[t]
            dst = g_at(u, row, n)
            src = acc.at[u % NB, pl.ds(aligned(row, 8), n)] if t == 3 else dst
            remote(src, dst, g_send.at[t, u % NS], g_recv.at[t, u], link(dims(u, p, t))[1]).start()

    def local_start(u):
        for p, (base, size) in enumerate(PARTS):
            n = size >> 3
            row = core * half + base + offs(u, p, size)[3]
            pltpu.make_async_copy(acc.at[u % NB, pl.ds(aligned(row, 8), n)], g_at(u, row, n), loc_sem.at[u % NS]).start()

    def local_wait(u):
        n = half >> 3
        pltpu.make_async_copy(acc.at[0, pl.ds(0, n)], g_hbm.at[pl.ds(0, n), pl.ds(0, TW)], loc_sem.at[u % NS]).wait()

    n_attn = seqs * pairs
    n_early = pairs + 2 * (seqs - 1)

    def place(a):
        b, c = a - pairs, a - n_early
        s = jnp.where(a < pairs, 0, 1 + jnp.where(c < 0, b // 2, c % (seqs - 1)))
        p = jnp.where(a < pairs, a, jnp.where(c < 0, b % 2, 2 + c // (seqs - 1)))
        return s, p, seq_rows(s), pl.ds(aligned(p * TW, TW), TW)

    def seq_rows(c):
        return pl.ds(aligned(c * seq, seq), seq)

    def attn_in(a, fn):
        _, _, rows, cols = place(a)
        sl = a % 2
        fn(pltpu.make_async_copy(qkv.at[:, rows, cols], qkv_v.at[sl], in_sem.at[0, sl]))
        fn(pltpu.make_async_copy(w_out.at[cols], o_c.at[sl], in_sem.at[1, sl]))

    def start(copy):
        copy.start()

    def wait(copy):
        copy.wait()

    def dproj_rows(a):
        s, p, _, _ = place(a)
        return dproj_v.at[p % 2, :, seq_rows(jnp.where(jnp.logical_and(s == 0, p >= 2), seqs - 1, s))]

    def attn_out(a):
        _, _, rows, cols = place(a)
        sl = a % 2
        return (pltpu.make_async_copy(o_v.at[sl], o_hbm.at[rows, cols], out_sem.at[0, sl]),
                pltpu.make_async_copy(o_t_v.at[sl], o_t_hbm.at[cols, rows], out_sem.at[1, sl]),
                pltpu.make_async_copy(dproj_rows(a), dproj_hbm.at[:, rows, cols], out_sem.at[2, sl]))

    def attn_out_wait(a):
        for c in attn_out(a):
            c.wait()

    def attn_step(a):
        @pl.when(jnp.logical_and(a != pairs - 1, a + 1 < n_attn))
        def _():
            attn_in(a + 1, start)

        attn_in(a, wait)

        @pl.when(jnp.logical_and(a >= 2, a // 2 != pairs // 2))
        def _():
            attn_out_wait(a)

        s, _, _, _ = place(a)
        sl = a % 2

        @pl.when(s == 0)
        def _():
            do_v[sl] = dot_nt(h_v[...], o_c[sl]).astype(BF)

        @pl.when(jnp.logical_and(s > 0, s < seqs - 1))
        def _():
            total = None
            for n in range(per):
                cols = slice(n * TN, (n + 1) * TN)
                part = dot_nt(wbuf[s - 1, cols], o_c[sl, :, cols])
                total = part if total is None else total + part
            do_v[sl] = total.astype(BF)

        @pl.when(s == seqs - 1)
        def _():
            do_v[sl] = dot_nt(dh_v[...].reshape(seq, dim), o_c[sl]).astype(BF)

        attend(scale, qkv_v.at[sl], do_v.at[sl], tabs, o_v.at[sl], o_t_v.at[sl], dproj_rows(a))
        for c in attn_out(a):
            c.start()

    def first_seq(p):
        rows = seq_rows(0)
        return pltpu.make_async_copy(dproj_hbm.at[:, rows, pl.ds(aligned(p * TW, TW), TW)], dproj_v.at[p % 2, :, rows], c0_sem.at[p % 2])

    def rhs_copy(u):
        j = u - n_qkv
        return pltpu.make_async_copy(do_seq.at[:, pl.ds(aligned(j * TW, TW), TW)], dproj_v.at[0, j % 3], rhs_sem.at[j % 3])

    def dw_tile(u):
        @pl.when(u == n_qkv)
        def _():
            pltpu.make_async_copy(o_t_hbm, lhs, lhs_sem).wait()

        @pl.when(u >= n_qkv)
        def _():
            rhs_copy(u).wait()

        @pl.when(jnp.logical_and(u % 3 == 0, jnp.logical_and(u >= 6, u < n_qkv)))
        def _():
            first_seq(u // 3).wait()

        p = jnp.where(u < n_qkv, (u // 3) % 2, 0)

        @pl.loop(0, dim // 512)
        def _(b):
            rows = pl.ds(aligned(b * 512, 512), 512)
            acc[u % NB, rows] = dot_nn(lhs[rows], dproj_v[p, u % 3])

        rs_start(u, 0)

        @pl.when(u == n_qkv - 1)
        def _():
            pltpu.make_async_copy(o_t_hbm, lhs, lhs_sem).start()

        @pl.when(jnp.logical_and(u + 2 >= n_qkv, u + 2 < n_all))
        def _():
            rhs_copy(u + 2).start()

    n_blocks = 4 * seqs

    def columns(n):
        return pl.ds(aligned(n * TN, TN), TN)

    def block(b):
        is_out = jnp.logical_or(b == 0, jnp.logical_and((b + 1) % 3 == 0, b <= 3 * seqs - 4))
        done = jnp.minimum((b + 1) // 3, seqs - 1)
        return is_out, done, b - 1 - done

    def tile_start(t):
        b, n, sl = t // per, t % per, t % 2
        is_out, c, q = block(b)

        @pl.when(is_out)
        def _():
            pltpu.make_async_copy(w_out.at[:, columns(n)], wbuf.at[sl], w_sem.at[0, sl]).start()
            pltpu.make_async_copy(h_seq.at[seq_rows(c), columns(n)], pbuf.at[sl], w_sem.at[1, sl]).start()

        @pl.when(jnp.logical_not(is_out))
        def _():
            pltpu.make_async_copy(w_qkv.at[:, columns((q % 3) * per + n)], wbuf.at[sl], w_sem.at[0, sl]).start()
            pltpu.make_async_copy(dproj_hbm.at[q % 3, seq_rows(q // 3), columns(n)], pbuf.at[sl], w_sem.at[1, sl]).start()

    def tile_wait(t):
        sl = t % 2
        pltpu.make_async_copy(w_out.at[:, columns(0)], wbuf.at[sl], w_sem.at[0, sl]).wait()
        pltpu.make_async_copy(h_seq.at[seq_rows(0), columns(0)], pbuf.at[sl], w_sem.at[1, sl]).wait()

    def o_load(c):
        n = seq // 2
        return [pltpu.make_async_copy(o_hbm.at[pl.ds(aligned(c * seq + k * n, n), n)], o_c.at[k], o_sem.at[k]) for k in range(2)]

    def y_sent(n):
        r = y_all.at[pl.ds(0, group - 1), :, columns(0)]
        return remote(r, r, y_send.at[n], y_recv.at[0], mate)

    def y_own_copy(c, n):
        return pltpu.make_async_copy(y_t.at[n, me], y_all.at[me * seqs + c, :, columns(n)], y_own.at[n])

    def out_tile(c, n, sl):
        y = pbuf[sl].astype(F32) + dot_nn(o_c[...].reshape(seq, dim), wbuf[sl])

        @pl.when(c > 0)
        def _():
            y_sent(n).wait_send()
            y_own_copy(0, n).wait()

        y_t[n] = y.astype(BF).reshape(group, loc, TN)
        for j in ORDER:
            peer = flipped(me, j)
            remote(y_t.at[n, peer], y_all.at[me * seqs + c, :, columns(n)], y_send.at[n], y_recv.at[c], peer).start()
        y_own_copy(c, n).start()

    def run_block(b):
        is_out, c_out, q = block(b)
        c, third = q // 3, q % 3

        @pl.when(is_out)
        def _():
            for x in o_load(c_out):
                x.wait()

        @pl.when(jnp.logical_and(jnp.logical_not(is_out), third == 2))
        def _():
            pltpu.make_async_copy(h_seq.at[seq_rows(c)], h_v, dh_sem.at[0]).start()
            pltpu.make_async_copy(do_seq.at[seq_rows(c)], dout_v, dh_sem.at[1]).start()

        @pl.loop(0, per)
        def _(n):
            t = b * per + n
            sl = t % 2

            @pl.when(jnp.logical_and(t != per - 1, t + 1 < n_blocks * per))
            def _():
                tile_start(t + 1)

            tile_wait(t)

            @pl.when(is_out)
            def _():
                out_tile(c_out, n, sl)

            @pl.when(jnp.logical_not(is_out))
            def _():
                part = dot_nt(pbuf[sl], wbuf[sl])
                first = jnp.logical_and(third == 0, n == 0)

                @pl.when(first)
                def _():
                    dn_acc[...] = part

                @pl.when(jnp.logical_not(first))
                def _():
                    dn_acc[...] += part

        @pl.when(jnp.logical_and(is_out, jnp.logical_and(c_out > 0, c_out + 1 < seqs)))
        def _():
            for x in o_load(c_out + 1):
                x.start()

        @pl.when(jnp.logical_and(jnp.logical_not(is_out), third == 2))
        def _():
            norm_back(c)

    def norm_back(c):
        pltpu.make_async_copy(h_seq.at[seq_rows(c)], h_v, dh_sem.at[0]).wait()
        pltpu.make_async_copy(do_seq.at[seq_rows(c)], dout_v, dh_sem.at[1]).wait()

        @pl.when(c > 0)
        def _():
            pltpu.make_async_copy(dh_v, dh_hbm.at[:, 0], dh_sem.at[2]).wait()

        gain = gain_ref[...].astype(F32)

        @pl.loop(0, group)
        def _(b):
            r = pl.ds(aligned(b * loc, loc), loc)
            h = h_v[r].astype(F32)
            inv = lax.rsqrt(jnp.mean(h * h, axis=-1, keepdims=True) + NORM_EPS)
            dn = dn_acc[r].astype(BF).astype(F32)
            dg = jnp.sum(dn * h * inv, axis=0, keepdims=True)
            ds = dn * gain
            dh = dout_v[r].astype(F32) + inv * ds - h * (inv * inv * inv) * jnp.mean(ds * h, axis=-1, keepdims=True)
            dh_v[b] = dh.astype(BF)
            first = jnp.logical_and(c == 0, b == 0)

            @pl.when(first)
            def _():
                dg_all[me] = dg

            @pl.when(jnp.logical_not(first))
            def _():
                dg_all[me] += dg

        @pl.when(c < by_xla)
        def _():
            pltpu.make_async_copy(dh_v, dh_hbm.at[:, c], dh_sem.at[2]).start()

        @pl.when(c >= by_xla)
        def _():
            pltpu.make_async_copy(dh_v, dh_loc.at[:, c - by_xla], dh_sem.at[2]).start()

    def dh_send(q):
        k, cols = q // 4, pl.ds(aligned((q % 4) * (dim // 4), dim // 4), dim // 4)
        for j in ORDER:
            peer = flipped(me, j)
            remote(dh_loc.at[peer, k, :, cols], dh_all.at[me, k, :, cols], x_send.at[q], x_recv.at[q], peer).start()
        pltpu.make_async_copy(dh_loc.at[me, k, :, cols], dh_all.at[me, k, :, cols], own_sem.at[q]).start()

    def dh_wait(q):
        r = dh_all.at[pl.ds(0, group - 1), 0, :, pl.ds(0, dim // 4)]
        done = remote(r, r, x_send.at[q], x_recv.at[q], mate)
        done.wait_recv()
        done.wait_send()
        pltpu.make_async_copy(dh_loc.at[0, 0, :, pl.ds(0, dim // 4)], dh_all.at[0, 0, :, pl.ds(0, dim // 4)], own_sem.at[q]).wait()

    def my_rows(c):
        return pl.ds(aligned(c * seq + me * loc, loc), loc)

    def from_all(dst, ss, rs):
        r = dst.at[pl.ds(0, (group - 1) * loc)]
        return remote(r, r, ss, rs, mate)

    def send_all(src, dst, ss, rs, c):
        for j in ORDER:
            peer = flipped(me, j)
            to = dh_v.at[me] if dst is do_seq and c == seqs - 1 else dst.at[my_rows(c)]
            remote(src.at[peer * seqs + c], to, ss.at[c], rs.at[c], peer).start()

    def project(c):
        rows = seq_rows(c)
        from_all(h_seq, h_send.at[c], h_recv.at[c]).wait_recv()
        load = pltpu.make_async_copy(h_seq.at[rows], h_v, ld_sem)
        load.start()
        load.wait()
        gain = gain_ref[...].astype(F32)
        blk = 128

        @pl.loop(0, seq // blk)
        def _(b):
            r = pl.ds(aligned(b * blk, blk), blk)
            h = h_v[r].astype(F32)
            inv = lax.rsqrt(jnp.mean(h * h, axis=-1, keepdims=True) + NORM_EPS)
            n = (h * inv * gain).astype(BF)
            dout_v[r] = n
            lhs[:, pl.ds(aligned(c * seq + b * blk, blk), blk)] = n.T

        @pl.loop(0, 3 * per)
        def _(n):
            t = c * 3 * per + n
            sl = t % 2

            @pl.when(t + 1 < seqs * 3 * per)
            def _():
                qkv_w(t + 1).start()

            qkv_w(t).wait()
            proj = dot_nn(dout_v[...], wbuf[sl])

            @pl.when(t >= 2)
            def _():
                qkv_out(t).wait()

            @pl.when(n < 2 * per)
            def _():
                for h in range(TN // 128):
                    cols = slice(h * 128, (h + 1) * 128)
                    pbuf[sl, :, cols] = rotate(proj[:, cols], tabs[:, :128], tabs[:, 128:]).astype(BF)

            @pl.when(n >= 2 * per)
            def _():
                pbuf[sl] = proj.astype(BF)

            qkv_out(t).start()

    def qkv_w(t):
        return pltpu.make_async_copy(w_qkv.at[:, columns(t % (3 * per))], wbuf.at[t % 2], w_sem.at[0, t % 2])

    def qkv_out(t):
        n = t % (3 * per)
        return pltpu.make_async_copy(pbuf.at[t % 2], qkv.at[n // per, seq_rows(t // (3 * per)), columns(n % per)], w_sem.at[1, t % 2])

    def gradient_in():
        for t in range(2):
            qkv_out(t).wait()
        attn_in(0, start)
        for c in range(seqs - 1):
            from_all(do_seq, d_send.at[c], d_recv.at[c]).wait_recv()
            rows = seq_rows(c)
            if c == 0:
                loads = [pltpu.make_async_copy(do_seq.at[rows], h_v, ld_sem)]
            else:
                loads = [pltpu.make_async_copy(do_seq.at[rows, pl.ds(n * TN, TN)], wbuf.at[c - 1, pl.ds(n * TN, TN)], x_send.at[n]) for n in range(per)]
            for x in loads:
                x.start()
            for x in loads:
                x.wait()
            if c == 0:
                pl.loop(0, pairs)(attn_step)
                attn_out_wait(pairs - 2)
                attn_out_wait(pairs - 1)
                for x in o_load(0):
                    x.start()
                tile_start(0)
                run_block(0)
                attn_in(pairs, start)
            else:
                pl.loop(pairs + 2 * c - 2, pairs + 2 * c)(attn_step)
        from_all(do_seq, d_send.at[seqs - 1], d_recv.at[seqs - 1]).wait_recv()
        last_copy().start()
        attn_step(n_early - 2)

    def last_copy():
        dst = do_seq.at[seq_rows(seqs - 1)]
        return pltpu.make_async_copy(dh_v, dst.reshape(group, loc, dim), ld_sem)

    by_xla = dh_hbm.shape[1]

    def own_in(k):
        src = hidden if k < seqs else d_out
        to = dh_v.at[me] if k == 2 * seqs - 1 else dout_v.at[pl.ds(k * loc, loc)]
        return pltpu.make_async_copy(src.at[me * seqs + k % seqs], to, own_sem.at[k])

    def own_out(k):
        dst = h_seq if k < seqs else do_seq
        return pltpu.make_async_copy(dout_v.at[pl.ds(k * loc, loc)], dst.at[my_rows(k % seqs)], own_sem.at[k])

    for k in range(2 * seqs):
        own_in(k).start()
    cos, sin = cos_ref[...], sin_ref[...]
    tab[...] = jnp.concatenate([cos, cos, -sin, sin], axis=1)
    barrier = pltpu.get_barrier_semaphore()
    for j in range(1, group):
        pl.semaphore_signal(barrier, inc=1, device_id=(flipped(me, j),), device_id_type=MESH)
    pl.semaphore_wait(barrier, group - 1)
    mine = pl.ds(aligned(me * loc, loc), loc)
    for j in ORDER:
        remote(tab, tabs.at[mine], t_send, t_recv, flipped(me, j)).start()
    for c in range(seqs):
        send_all(hidden, h_seq, h_send, h_recv, c)
    for c in range(seqs):
        send_all(d_out, do_seq, d_send, d_recv, c)
    for k in range(2 * seqs):
        own_in(k).wait()
        if k < 2 * seqs - 1:
            own_out(k).start()
    tabs[mine] = tab[...]
    from_all(tabs, t_send, t_recv).wait_recv()
    for k in range(2 * seqs - 1):
        own_out(k).wait()
    qkv_w(0).start()
    pl.loop(0, seqs)(project)
    gradient_in()

    first_out = 3 * (pairs - 1)
    first_dn = first_out + seqs

    def step(i, carry):
        def guarded(lag, fn):
            u = i - lag

            @pl.when(jnp.logical_and(u >= 0, u < n_all))
            def _():
                fn(u)

        def ag0(u):
            ag_all(u, 0).wait_recv()

        def ag1(u):
            ag_all(u, 1).wait_recv()
            ag_start(u, 0)

        def ag2(u):
            ag_all(u, 2).wait_recv()
            ag_start(u, 1)

        def ag3(u):
            ag_all(u, 3).wait_recv()
            ag_all(u, 3).wait_send()
            local_wait(u)
            ag_start(u, 2)

        def last(u):
            rs_finish(u, 3)
            local_start(u)
            ag_start(u, 3)

        def middle(t):
            def fn(u):
                rs_finish(u, t)
                rs_start(u, t + 1)
            return fn

        for lag, fn in enumerate((dw_tile, middle(0), middle(1), middle(2), last, ag3, ag2, ag1, ag0)):
            guarded(lag, fn)

        from_a, to_a = [n_early - 1 + jnp.maximum(k - 2, 0) for k in (i, i + 1)]

        @pl.when(jnp.logical_and(i % 3 == 0, jnp.logical_and(i >= 3, i < first_out)))
        def _():
            first_seq(i // 3 + 1).start()

        @pl.when(i < first_out)
        def _():
            pl.loop(from_a, to_a)(attn_step)

        @pl.when(i == first_out)
        def _():
            attn_out_wait(n_attn - 2)
            attn_out_wait(n_attn - 1)
            for x in o_load(1):
                x.start()
            tile_start(per)

        def blocks(i):
            k = i - first_out
            return jnp.where(k <= seqs, jnp.maximum(3 * k - 1, 1), jnp.minimum(k + 2 * seqs - 1, n_blocks))

        @pl.when(i >= first_out)
        def _():
            pl.loop(blocks(i), blocks(i + 1))(run_block)

        @pl.when(i == 3)
        def _():
            last_copy().wait()

        first_dh = first_dn + seqs + 1

        @pl.when(i == first_dh)
        def _():
            pltpu.make_async_copy(dh_v, dh_hbm.at[:, 0], dh_sem.at[2]).wait()
            for j in range(1, group):
                remote(dg_all.at[me], dg_all.at[me], dg_send, dg_recv, flipped(me, j)).start()

        @pl.when(jnp.logical_and(i >= first_dh, i < first_dh + 4 * (seqs - by_xla)))
        def _():
            dh_send(i - first_dh)

        return carry

    lax.fori_loop(0, n_all + 8, step, 0)

    for c in range(seqs):
        r = y_all.at[pl.ds(0, group - 1)]
        remote(r, r, y_send.at[0], y_recv.at[c], mate).wait_recv()
        from_all(h_seq, h_send.at[c], h_recv.at[c]).wait_send()
        from_all(do_seq, d_send.at[c], d_recv.at[c]).wait_send()
    for n in range(per):
        y_sent(n).wait_send()
        y_own_copy(0, n).wait()
    from_all(tabs, t_send, t_recv).wait_send()
    for q in range(4 * (seqs - by_xla)):
        dh_wait(q)
    others = remote(dg_all.at[pl.ds(0, group - 1)], dg_all.at[pl.ds(0, group - 1)], dg_send, dg_recv, mate)
    others.wait_recv()
    others.wait_send()
    dgain = dg_all[0]
    for j in range(1, group):
        dgain = dgain + dg_all[j]
    dgain_ref[...] = dgain
    for j in range(NS):
        u = n_all - NS + j
        for t in range(4):
            pl.semaphore_wait(credit.at[t, u % NS], 1 if t == 0 else 3)
            if t < 3:
                ag_all(u, t).wait_send()


BY_XLA = 2


def main_call(hidden, d_out, cos_tab, sin_tab, w_qkv, w_out, gain):
    n, loc, dim = hidden.shape
    group = 16
    rows = n * loc
    seqs = n // group
    seq = loc * group
    h = dim // 2
    n_all = 4 * dim // TW
    hbm = pl.BlockSpec(memory_space=pl.ANY)
    vmem = pl.BlockSpec(memory_space=pltpu.VMEM)
    D = pltpu.SemaphoreType.DMA
    S = jax.ShapeDtypeStruct
    V = pltpu.VMEM
    act = S((rows, dim), BF)
    return pl.pallas_call(
        functools.partial(main_kernel, 128 ** -0.5),
        in_specs=[hbm] * 2 + [vmem] * 2 + [hbm] * 2 + [vmem],
        out_specs=[hbm] * 11 + [vmem],
        out_shape=[S((dim, 4 * dim), F32), act, act, S((3, rows, dim), BF),
                   act, S((dim, rows), BF), S((3, rows, dim), BF), S((n, loc, dim), BF),
                   S((group, BY_XLA, loc, dim), BF), S((group, seqs - BY_XLA, loc, dim), BF), S((group, seqs - BY_XLA, loc, dim), BF), S((1, dim), F32)],
        scratch_shapes=[
            V((dim, rows), BF), V((2, 3, rows, TW), BF), V((NB, dim, TW), F32),
            V((NS, h, TW), F32), V((NS, h >> 1, TW), F32), V((NS, h >> 2, TW), F32), V((NS, h >> 3, TW), F32),
            V((2, 3, seq, TW), BF), V((2, seq, TW), BF), V((2, seq, TW), BF), V((2, TW, seq), BF), V((seq, 256), F32), V((loc, 256), F32),
            V((seq, dim), F32), V((seq, dim), BF), V((seq, dim), BF), V((group, loc, dim), BF), V((group, 1, dim), F32),
            V((2, dim, 512), BF), V((2, seq, 512), BF), V((2, seq // 2, dim), BF), V((dim // 512, group, loc, 512), BF),
            D, D, D((4, NS)), D((4, NS)), pltpu.SemaphoreType.REGULAR((4, NS)), D((NS,)), D((4, NS)), D((4, n_all)),
            D((2, 2)), D((3, 2)), D((3,)), D((3,)), D, D, D((2, 2)), D((2,)), D((2,)),
            D((seqs,)), D((seqs,)), D((seqs,)), D((seqs,)), D, D, D((2 * seqs,)), D((dim // 512,)), D((seqs,)), D((dim // 512,)), D((4 * (seqs - BY_XLA),)), D((4 * (seqs - BY_XLA),)),
        ],
        compiler_params=pltpu.CompilerParams(collective_id=0, has_side_effects=True, vmem_limit_bytes=67043328),
        cost_estimate=pl.CostEstimate(flops=28 * rows * dim * dim, bytes_accessed=90 * dim * dim, transcendentals=0),
        name="main",
    )(hidden, d_out, cos_tab, sin_tab, w_qkv, w_out, gain)


def place_kernel(y_in, b_in, y_out, dh_out):
    y_out[...] = y_in[...]
    dh_out[...] = b_in[...]


def place_call(y, b):
    n, loc, dim = y.shape
    group, k = b.shape[:2]
    seqs = n // group
    return pl.pallas_call(
        place_kernel,
        grid=(4,),
        in_specs=[pl.BlockSpec((n // 4, loc, dim), lambda j: (j, 0, 0)), pl.BlockSpec((group // 4, k, loc, dim), lambda j: (j, 0, 0, 0))],
        out_specs=[pl.BlockSpec((n // 4, loc, dim), lambda j: (j, 0, 0)), pl.BlockSpec((group // 4, k, loc, dim), lambda j: (j, seqs // k - 1, 0, 0))],
        out_shape=[jax.ShapeDtypeStruct((n, loc, dim), BF), jax.ShapeDtypeStruct((group, seqs, loc, dim), BF)],
        cost_estimate=pl.CostEstimate(flops=8 * n * loc * dim, bytes_accessed=6 * n * loc * dim, transcendentals=0),
        name="place",
    )(y, b)


def fill_kernel(a_in, dh_in, dh_out):
    dh_out[...] = a_in[...]


def fill_call(a, dh):
    group, k, loc, dim = a.shape
    return pl.pallas_call(
        fill_kernel,
        grid=(4,),
        in_specs=[pl.BlockSpec((group // 4, k, loc, dim), lambda j: (j, 0, 0, 0)), pl.BlockSpec(memory_space=pl.ANY)],
        out_specs=pl.BlockSpec((group // 4, k, loc, dim), lambda j: (j, 0, 0, 0)),
        out_shape=jax.ShapeDtypeStruct(dh.shape, BF),
        input_output_aliases={1: 0},
        name="fill",
    )(a, dh)


def solution(mesh):
    group = mesh.shape['sp']
    token_spec = P(None, 'sp', None)
    table_spec = P('sp', None)

    def device_step(hidden, norm_gain, w_qkv, w_out, cos_tab, sin_tab, d_out):
        num_seqs, local_len, dim = hidden.shape
        gain = norm_gain.reshape(1, dim)
        dw, _, _, _, _, _, _, y, dh_a, _, dh_b, dgain = main_call(hidden, d_out, cos_tab, sin_tab, w_qkv, w_out, gain)
        dh_a = lax.all_to_all(dh_a, 'sp', split_axis=0, concat_axis=0, tiled=True)
        y, dh = place_call(y, dh_b)
        dh = fill_call(dh_a, dh).reshape(num_seqs, local_len, dim)
        return y, dh, dw[:, :3 * dim], dw[:, 3 * dim:], dgain.reshape(dim)

    return jax.shard_map(device_step, mesh=mesh, in_specs=(token_spec, P(), P(), P(), table_spec, table_spec, token_spec), out_specs=(token_spec, token_spec, P(), P(), P()), check_vma=False)
```

time: 947 us -> 839 us (0.89)
  blocking collectives: 97.9 us -> 0 us
  Pallas kernels: 712 us -> 784 us
  waiting for transfers between devices: 60.6 us -> 0.01 us
  local copies, waits for them, and re-layouts: 65.3 us -> 48.2 us
    pallas_call x1, Pallas kernels: 507 us -> 770 us  [main_call(): pl.pallas_call(functools.partial(main_kernel, 128 ** (-0.5)), in_specs=[h...]
    pallas_call x1 -> x2, Pallas kernels: 205 us -> 14 us  [the longest x1 9.25 us: place_call(): pl.pallas_call(place_kernel, grid=(4,), in_specs=[pl.BlockSpec((n // 4, l...]
    all_to_all x1 -> x0, blocking collectives: 97.9 us -> none  [to_tokens(): x = lax.all_to_all(x, 'sp', split_axis=0, concat_axis=0, tiled=True)]
    all_to_all x1, waiting for transfers between devices: 60.6 us -> 0.01 us  [device_step(): dh_a = lax.all_to_all(dh_a, 'sp', split_axis=0, concat_axis=0, tiled=True)]
    unnamed x9 -> x3, local copies, waits for them, and re-layouts: 18.3 us -> 0.6 us
  transfers between devices with their start and end apart: 1 -> 1, of which waited for: 1 -> 0; matrix products, arithmetic and copies ran while one was open for 5% -> 6% of each run, Pallas kernels for 0% -> 1%
where the time goes in v3:
time: 839 us; the launch traced here: 836 us
  Pallas kernels  784 us (93%)
  local copies, waits for them, and re-layouts  48.2 us (6%)
    pallas_call x1, Pallas kernels, main_call(): pl.pallas_call(functools.partial(main_kernel, 128 ** (-0.5)), in_specs=[h...  770 us
    slice x2, local copies, waits for them, and re-layouts, device_step(): return (y, dh, dw[:, :3 * dim], dw[:, 3 * dim:], dgain.reshape(dim))  46.3 us
  transfers between devices with their start and end apart: 1, of which 0 were waited for; matrix products, arithmetic and copies ran while one was open for 6% of the time, Pallas kernels for 1%

profile of v3, /device:TPU:0, one launch (start us, length us, event | category | flops | bytes accessed | tf_op | source)
XLA Modules:
  0.0 836.2 jit_solution(779221451123769190)
XLA Ops:
  0.6 1.3 reshape.19.gain_ref
  1.9 770.0 %main.1 = (f32[2048,8192]{1,0:T(8,128)}, bf16[2048,2048]{1,0:T(8,128)(2,1)}, bf16[2048,2048]{1,0:T(8,128)(2,1)}, bf16[3,2048,2048]{2,1,0:T(8,128)(2,1)}, bf16[20...) custom-call(bf16[64,32,2048]{2,1,0:T(8,128)(2,1)} %hidden.1, ...), custom_call_target="tpu_custom_call" | custom-call | flops 240518168576 | bytes 377487360 | tf_op jit(solution)/shard_map/main/pallas_call | solution.py:757
  772.0 3.3 all-to-all-start
  775.3 11.8 %slice.7 = f32[2048,2048]{1,0:T(8,128)} slice(f32[2048,8192]{1,0:T(8,128)} %get-tuple-element.17), slice={[0:2048], [6144:8192]} | slice | bytes 33554432 | tf_op jit(solution)/shard_map/slice | solution.py:829
  787.1 34.5 %slice.6 = f32[2048,6144]{1,0:T(8,128)} slice(f32[2048,8192]{1,0:T(8,128)} %get-tuple-element.17), slice={[0:2048], [0:6144]} | slice | bytes 100663296 | tf_op jit(solution)/shard_map/slice | solution.py:829
  821.6 9.3 %place.1 = (bf16[64,32,2048]{2,1,0:T(8,128)(2,1)}, bf16[16,4,32,2048]{3,2,1,0:T(8,128)(2,1)}) custom-call(bf16[64,32,2048]{2,1,0:T(8,128)(2,1)} %get-tuple-element.12.y_in, bf16[16,2,32,2048]{3,2,1,0:T(8,128)(2,1)} %get-tuple-element.13.b_in), custom_call_target="tpu_custom_call" | custom-call | flops 33554432 | bytes 25165824 | tf_op jit(solution)/shard_map/place/pallas_call | solution.py:789
  830.9 0.0 all-to-all-done.a_in
  830.9 0.0 copy-start
  830.9 4.7 fill.1
  835.6 0.0 copy-done
  835.6 0.6 copy.15
Async XLA Ops:
  772.0 58.9 %all-to-all-start = ((bf16[16,2,32,2048]{3,2,1,0:T(8,128)(2,1)}), bf16[16,2,32,2048]{3,2,1,0:T(8,128)(2,1)}, u32[]{:S(2)}, u32[]{:S(2)}) async-start(bf16[16,2,32,2048]{3,2,1,0:T(8,128)(2,1)} %get-tuple-element.15), calls=%async_computation | async-start | bytes 8388608 | tf_op jit(solution)/shard_map/all_to_all | solution.py:826
  830.9 4.7 copy-start

commit v4 on v3

--- a/solution.py
+++ b/solution.py
@@ -313,12 +313,15 @@
 
         p = jnp.where(u < n_qkv, (u // 3) % 2, 0)
 
-        @pl.loop(0, dim // 512)
-        def _(b):
-            rows = pl.ds(aligned(b * 512, 512), 512)
-            acc[u % NB, rows] = dot_nn(lhs[rows], dproj_v[p, u % 3])
-
+        def half_tile(mine):
+            @pl.loop(0, half // TN)
+            def _(b):
+                rows = pl.ds(aligned(mine * half + b * TN, TN), TN)
+                acc[u % NB, rows] = dot_nn(lhs[rows], dproj_v[p, u % 3])
+
+        half_tile(1 - core)
         rs_start(u, 0)
+        half_tile(core)
 
         @pl.when(u == n_qkv - 1)
         def _():
@@ -441,7 +444,7 @@
         def _():
             pltpu.make_async_copy(dh_v, dh_hbm.at[:, 0], dh_sem.at[2]).wait()
 
-        gain = gain_ref[...].astype(F32)
+        gain = gain_ref[...].astype(F32).reshape(1, dim)
 
         @pl.loop(0, group)
         def _(b):
@@ -504,7 +507,7 @@
         load = pltpu.make_async_copy(h_seq.at[rows], h_v, ld_sem)
         load.start()
         load.wait()
-        gain = gain_ref[...].astype(F32)
+        gain = gain_ref[...].astype(F32).reshape(1, dim)
         blk = 128
 
         @pl.loop(0, seq // blk)
@@ -662,10 +665,9 @@
                 rs_start(u, t + 1)
             return fn
 
-        for lag, fn in enumerate((dw_tile, middle(0), middle(1), middle(2), last, ag3, ag2, ag1, ag0)):
-            guarded(lag, fn)
-
-        from_a, to_a = [n_early - 1 + jnp.maximum(k - 2, 0) for k in (i, i + 1)]
+        guarded(0, dw_tile)
+
+        from_a, to_a = [n_early - 1 + jnp.where(k > 2, k - 1, 0) for k in (i, i + 1)]
 
         @pl.when(jnp.logical_and(i % 3 == 0, jnp.logical_and(i >= 3, i < first_out)))
         def _():
@@ -673,7 +675,10 @@
 
         @pl.when(i < first_out)
         def _():
-            pl.loop(from_a, to_a)(attn_step)
+            pl.loop(from_a, jnp.minimum(to_a, n_attn))(attn_step)
+
+        for lag, fn in enumerate((middle(0), middle(1), middle(2), last, ag3, ag2, ag1, ag0)):
+            guarded(lag + 1, fn)
 
         @pl.when(i == first_out)
         def _():
@@ -685,7 +690,7 @@
 
         def blocks(i):
             k = i - first_out
-            return jnp.where(k <= seqs, jnp.maximum(3 * k - 1, 1), jnp.minimum(k + 2 * seqs - 1, n_blocks))
+            return jnp.where(k <= seqs, jnp.maximum(3 * k - 1, 1), jnp.minimum(k + 2 * seqs, n_blocks))
 
         @pl.when(i >= first_out)
         def _():
@@ -695,7 +700,7 @@
         def _():
             last_copy().wait()
 
-        first_dh = first_dn + seqs + 1
+        first_dh = first_dn + seqs
 
         @pl.when(i == first_dh)
         def _():
@@ -728,7 +733,7 @@
     dgain = dg_all[0]
     for j in range(1, group):
         dgain = dgain + dg_all[j]
-    dgain_ref[...] = dgain
+    dgain_ref[...] = dgain.reshape(dim)
     for j in range(NS):
         u = n_all - NS + j
         for t in range(4):
@@ -760,7 +765,7 @@
         out_specs=[hbm] * 11 + [vmem],
         out_shape=[S((dim, 4 * dim), F32), act, act, S((3, rows, dim), BF),
                    act, S((dim, rows), BF), S((3, rows, dim), BF), S((n, loc, dim), BF),
-                   S((group, BY_XLA, loc, dim), BF), S((group, seqs - BY_XLA, loc, dim), BF), S((group, seqs - BY_XLA, loc, dim), BF), S((1, dim), F32)],
+                   S((group, BY_XLA, loc, dim), BF), S((group, seqs - BY_XLA, loc, dim), BF), S((group, seqs - BY_XLA, loc, dim), BF), S((dim,), F32)],
         scratch_shapes=[
             V((dim, rows), BF), V((2, 3, rows, TW), BF), V((NB, dim, TW), F32),
             V((NS, h, TW), F32), V((NS, h >> 1, TW), F32), V((NS, h >> 2, TW), F32), V((NS, h >> 3, TW), F32),
@@ -821,11 +826,10 @@
 
     def device_step(hidden, norm_gain, w_qkv, w_out, cos_tab, sin_tab, d_out):
         num_seqs, local_len, dim = hidden.shape
-        gain = norm_gain.reshape(1, dim)
-        dw, _, _, _, _, _, _, y, dh_a, _, dh_b, dgain = main_call(hidden, d_out, cos_tab, sin_tab, w_qkv, w_out, gain)
+        dw, _, _, _, _, _, _, y, dh_a, _, dh_b, dgain = main_call(hidden, d_out, cos_tab, sin_tab, w_qkv, w_out, norm_gain)
         dh_a = lax.all_to_all(dh_a, 'sp', split_axis=0, concat_axis=0, tiled=True)
         y, dh = place_call(y, dh_b)
         dh = fill_call(dh_a, dh).reshape(num_seqs, local_len, dim)
-        return y, dh, dw[:, :3 * dim], dw[:, 3 * dim:], dgain.reshape(dim)
+        return y, dh, dw[:, :3 * dim], dw[:, 3 * dim:], dgain
 
     return jax.shard_map(device_step, mesh=mesh, in_specs=(token_spec, P(), P(), P(), table_spec, table_spec, token_spec), out_specs=(token_spec, token_spec, P(), P(), P()), check_vma=False)

time: 839 us -> 837 us (level)
  no operation moved by 1% of the time
where the time goes in v4:
time: 837 us; the launch traced here: 834 us
  Pallas kernels  783 us (94%)
  local copies, waits for them, and re-layouts  46.9 us (6%)
    pallas_call x1, Pallas kernels, main_call(): pl.pallas_call(functools.partial(main_kernel, 128 ** (-0.5)), in_specs=[h...  769 us
    slice x2, local copies, waits for them, and re-layouts, device_step(): return (y, dh, dw[:, :3 * dim], dw[:, 3 * dim:], dgain)  46.3 us
  transfers between devices with their start and end apart: 1, of which 0 were waited for; matrix products, arithmetic and copies ran while one was open for 6% of the time, Pallas kernels for 1%

profile of v4, /device:TPU:0, one launch (start us, length us, event | category | flops | bytes accessed | tf_op | source)
XLA Modules:
  0.0 833.6 jit_solution(5460318862793146782)
XLA Ops:
  0.6 768.7 %main.1 = (f32[2048,8192]{1,0:T(8,128)}, bf16[2048,2048]{1,0:T(8,128)(2,1)}, bf16[2048,2048]{1,0:T(8,128)(2,1)}, bf16[3,2048,2048]{2,1,0:T(8,128)(2,1)}, bf16[20...) custom-call(bf16[64,32,2048]{2,1,0:T(8,128)(2,1)} %hidden.1, ...), custom_call_target="tpu_custom_call" | custom-call | flops 240518168576 | bytes 377487360 | tf_op jit(solution)/shard_map/main/pallas_call | solution.py:762
  769.4 3.3 all-to-all-start
  772.7 11.8 %slice.7 = f32[2048,2048]{1,0:T(8,128)} slice(f32[2048,8192]{1,0:T(8,128)} %get-tuple-element.17), slice={[0:2048], [6144:8192]} | slice | bytes 33554432 | tf_op jit(solution)/shard_map/slice | solution.py:833
  784.5 34.5 %slice.6 = f32[2048,6144]{1,0:T(8,128)} slice(f32[2048,8192]{1,0:T(8,128)} %get-tuple-element.17), slice={[0:2048], [0:6144]} | slice | bytes 100663296 | tf_op jit(solution)/shard_map/slice | solution.py:833
  819.0 9.3 %place.1 = (bf16[64,32,2048]{2,1,0:T(8,128)(2,1)}, bf16[16,4,32,2048]{3,2,1,0:T(8,128)(2,1)}) custom-call(bf16[64,32,2048]{2,1,0:T(8,128)(2,1)} %get-tuple-element.12.y_in, bf16[16,2,32,2048]{3,2,1,0:T(8,128)(2,1)} %get-tuple-element.13.b_in), custom_call_target="tpu_custom_call" | custom-call | flops 33554432 | bytes 25165824 | tf_op jit(solution)/shard_map/place/pallas_call | solution.py:794
  828.2 0.0 all-to-all-done.a_in
  828.3 0.0 copy-start
  828.3 4.7 fill.1
  833.0 0.0 copy-done
  833.0 0.6 copy.15
Async XLA Ops:
  769.4 58.9 %all-to-all-start = ((bf16[16,2,32,2048]{3,2,1,0:T(8,128)(2,1)}), bf16[16,2,32,2048]{3,2,1,0:T(8,128)(2,1)}, u32[]{:S(2)}, u32[]{:S(2)}) async-start(bf16[16,2,32,2048]{3,2,1,0:T(8,128)(2,1)} %get-tuple-element.15), calls=%async_computation | async-start | bytes 8388608 | tf_op jit(solution)/shard_map/all_to_all | solution.py:830
  828.3 4.7 copy-start

commit v5 on v4

--- a/solution.py
+++ b/solution.py
@@ -7,6 +7,7 @@
 from jax.sharding import PartitionSpec as P
 
 NORM_EPS = 1e-6
+HEAD = 128
 BF = jnp.bfloat16
 F32 = jnp.float32
 VMEM_LIMIT = 60 * 1024 * 1024
@@ -89,17 +90,17 @@
             o_out[rows, cols] = o_t.T.astype(BF)
             o_t_out[cols, rows] = o_t.astype(BF)
             dq = dq_t.T.astype(BF).astype(F32)
-            dproj_out[0, rows, cols] = unrotate(dq, tabs[rows, :128], tabs[rows, 128:]).astype(BF)
+            dproj_out[0, rows, cols] = unrotate(dq, tabs[rows, :HEAD], tabs[rows, HEAD:]).astype(BF)
         for j in range(seq // BLK):
             rows = slice(j * BLK, (j + 1) * BLK)
             dkj = dk[j].astype(BF).astype(F32)
-            dproj_out[1, rows, cols] = unrotate(dkj, tabs[rows, :128], tabs[rows, 128:]).astype(BF)
+            dproj_out[1, rows, cols] = unrotate(dkj, tabs[rows, :HEAD], tabs[rows, HEAD:]).astype(BF)
             dproj_out[2, rows, cols] = dv[j].astype(BF)
 
 
 def main_kernel(scale, hidden, d_out, cos_ref, sin_ref, w_qkv, w_out, gain_ref,
                 g_hbm, h_seq, do_seq, qkv, o_hbm, o_t_hbm, dproj_hbm, y_all, dh_hbm, dh_loc, dh_all, dgain_ref,
-                lhs, dproj_v, acc, r0, r1, r2, r3, qkv_v, do_v, o_v, o_t_v, tabs, tab, dn_acc, h_v, dout_v, dh_v, dg_all, wbuf, pbuf, o_c, y_t,
+                lhs, dproj_v, acc, r0, r1, r2, r3, qkv_v, do_v, o_v, o_t_v, tabs, tab, tab_all, dn_acc, h_v, dout_v, dh_v, dg_all, wbuf, pbuf, o_c, y_t,
                 lhs_sem, ld_sem, s_send, s_recv, credit, loc_sem, g_send, g_recv,
                 in_sem, out_sem, rhs_sem, dh_sem, dg_send, dg_recv, w_sem, o_sem, c0_sem,
                 h_send, h_recv, d_send, d_recv, t_send, t_recv, own_sem, y_send, y_recv, y_own, x_send, x_recv):
@@ -539,7 +540,7 @@
             def _():
                 for h in range(TN // 128):
                     cols = slice(h * 128, (h + 1) * 128)
-                    pbuf[sl, :, cols] = rotate(proj[:, cols], tabs[:, :128], tabs[:, 128:]).astype(BF)
+                    pbuf[sl, :, cols] = rotate(proj[:, cols], tabs[:, :HEAD], tabs[:, HEAD:]).astype(BF)
 
             @pl.when(n >= 2 * per)
             def _():
@@ -599,17 +600,18 @@
         dst = h_seq if k < seqs else do_seq
         return pltpu.make_async_copy(dout_v.at[pl.ds(k * loc, loc)], dst.at[my_rows(k % seqs)], own_sem.at[k])
 
+    barrier = pltpu.get_barrier_semaphore()
+    for j in reversed(ORDER):
+        pl.semaphore_signal(barrier, inc=1, device_id=(flipped(me, j),), device_id_type=MESH)
     for k in range(2 * seqs):
         own_in(k).start()
-    cos, sin = cos_ref[...], sin_ref[...]
-    tab[...] = jnp.concatenate([cos, cos, -sin, sin], axis=1)
-    barrier = pltpu.get_barrier_semaphore()
-    for j in range(1, group):
-        pl.semaphore_signal(barrier, inc=1, device_id=(flipped(me, j),), device_id_type=MESH)
+    qkv_w(0).start()
+    mine = pl.ds(aligned(me * loc, loc), loc)
+    tab[...] = jnp.concatenate([cos_ref[...], sin_ref[...]], axis=1)
+    tab_all[mine] = tab[...]
     pl.semaphore_wait(barrier, group - 1)
-    mine = pl.ds(aligned(me * loc, loc), loc)
     for j in ORDER:
-        remote(tab, tabs.at[mine], t_send, t_recv, flipped(me, j)).start()
+        remote(tab, tab_all.at[mine], t_send, t_recv, flipped(me, j)).start()
     for c in range(seqs):
         send_all(hidden, h_seq, h_send, h_recv, c)
     for c in range(seqs):
@@ -618,11 +620,14 @@
         own_in(k).wait()
         if k < 2 * seqs - 1:
             own_out(k).start()
-    tabs[mine] = tab[...]
-    from_all(tabs, t_send, t_recv).wait_recv()
+    from_all(tab_all, t_send, t_recv).wait_recv()
+    table = tab_all[...]
+    swapped = pltpu.roll(table, 64, 1)
+    left = lax.broadcasted_iota(jnp.int32, table.shape, 1) < 64
+    tabs[:, :HEAD] = jnp.where(left, table, swapped)
+    tabs[:, HEAD:] = jnp.where(left, -swapped, table)
     for k in range(2 * seqs - 1):
         own_out(k).wait()
-    qkv_w(0).start()
     pl.loop(0, seqs)(project)
     gradient_in()
 
@@ -724,7 +729,7 @@
     for n in range(per):
         y_sent(n).wait_send()
         y_own_copy(0, n).wait()
-    from_all(tabs, t_send, t_recv).wait_send()
+    from_all(tab_all, t_send, t_recv).wait_send()
     for q in range(4 * (seqs - by_xla)):
         dh_wait(q)
     others = remote(dg_all.at[pl.ds(0, group - 1)], dg_all.at[pl.ds(0, group - 1)], dg_send, dg_recv, mate)
@@ -769,7 +774,7 @@
         scratch_shapes=[
             V((dim, rows), BF), V((2, 3, rows, TW), BF), V((NB, dim, TW), F32),
             V((NS, h, TW), F32), V((NS, h >> 1, TW), F32), V((NS, h >> 2, TW), F32), V((NS, h >> 3, TW), F32),
-            V((2, 3, seq, TW), BF), V((2, seq, TW), BF), V((2, seq, TW), BF), V((2, TW, seq), BF), V((seq, 256), F32), V((loc, 256), F32),
+            V((2, 3, seq, TW), BF), V((2, seq, TW), BF), V((2, seq, TW), BF), V((2, TW, seq), BF), V((seq, 256), F32), V((loc, 128), F32), V((seq, 128), F32),
             V((seq, dim), F32), V((seq, dim), BF), V((seq, dim), BF), V((group, loc, dim), BF), V((group, 1, dim), F32),
             V((2, dim, 512), BF), V((2, seq, 512), BF), V((2, seq // 2, dim), BF), V((dim // 512, group, loc, 512), BF),
             D, D, D((4, NS)), D((4, NS)), pltpu.SemaphoreType.REGULAR((4, NS)), D((NS,)), D((4, NS)), D((4, n_all)),
@@ -793,9 +798,9 @@
     seqs = n // group
     return pl.pallas_call(
         place_kernel,
-        grid=(4,),
-        in_specs=[pl.BlockSpec((n // 4, loc, dim), lambda j: (j, 0, 0)), pl.BlockSpec((group // 4, k, loc, dim), lambda j: (j, 0, 0, 0))],
-        out_specs=[pl.BlockSpec((n // 4, loc, dim), lambda j: (j, 0, 0)), pl.BlockSpec((group // 4, k, loc, dim), lambda j: (j, seqs // k - 1, 0, 0))],
+        grid=(2,),
+        in_specs=[pl.BlockSpec((n // 2, loc, dim), lambda j: (j, 0, 0)), pl.BlockSpec((group // 2, k, loc, dim), lambda j: (j, 0, 0, 0))],
+        out_specs=[pl.BlockSpec((n // 2, loc, dim), lambda j: (j, 0, 0)), pl.BlockSpec((group // 2, k, loc, dim), lambda j: (j, seqs // k - 1, 0, 0))],
         out_shape=[jax.ShapeDtypeStruct((n, loc, dim), BF), jax.ShapeDtypeStruct((group, seqs, loc, dim), BF)],
         cost_estimate=pl.CostEstimate(flops=8 * n * loc * dim, bytes_accessed=6 * n * loc * dim, transcendentals=0),
         name="place",
@@ -810,9 +815,9 @@
     group, k, loc, dim = a.shape
     return pl.pallas_call(
         fill_kernel,
-        grid=(4,),
-        in_specs=[pl.BlockSpec((group // 4, k, loc, dim), lambda j: (j, 0, 0, 0)), pl.BlockSpec(memory_space=pl.ANY)],
-        out_specs=pl.BlockSpec((group // 4, k, loc, dim), lambda j: (j, 0, 0, 0)),
+        grid=(2,),
+        in_specs=[pl.BlockSpec((group // 2, k, loc, dim), lambda j: (j, 0, 0, 0)), pl.BlockSpec(memory_space=pl.ANY)],
+        out_specs=pl.BlockSpec((group // 2, k, loc, dim), lambda j: (j, 0, 0, 0)),
         out_shape=jax.ShapeDtypeStruct(dh.shape, BF),
         input_output_aliases={1: 0},
         name="fill",

time: 837 us -> 831 us (level)
  no operation moved by 1% of the time
where the time goes in v5:
time: 831 us; the launch traced here: 828 us
  Pallas kernels  777 us (94%)
  local copies, waits for them, and re-layouts  46.9 us (6%)
    pallas_call x1, Pallas kernels, main_call(): pl.pallas_call(functools.partial(main_kernel, 128 ** (-0.5)), in_specs=[h...  764 us
    slice x2, local copies, waits for them, and re-layouts, device_step(): return (y, dh, dw[:, :3 * dim], dw[:, 3 * dim:], dgain)  46.3 us
  transfers between devices with their start and end apart: 1, of which 0 were waited for; matrix products, arithmetic and copies ran while one was open for 6% of the time, Pallas kernels for 1%

profile of v5, /device:TPU:0, one launch (start us, length us, event | category | flops | bytes accessed | tf_op | source)
XLA Modules:
  0.0 827.7 jit_solution(11330377712372966973)
XLA Ops:
  0.6 764.3 %main.1 = (f32[2048,8192]{1,0:T(8,128)}, bf16[2048,2048]{1,0:T(8,128)(2,1)}, bf16[2048,2048]{1,0:T(8,128)(2,1)}, bf16[3,2048,2048]{2,1,0:T(8,128)(2,1)}, bf16[20...) custom-call(bf16[64,32,2048]{2,1,0:T(8,128)(2,1)} %hidden.1, ...), custom_call_target="tpu_custom_call" | custom-call | flops 240518168576 | bytes 377487360 | tf_op jit(solution)/shard_map/main/pallas_call | solution.py:767
  765.0 3.3 all-to-all-start
  768.3 11.8 %slice.7 = f32[2048,2048]{1,0:T(8,128)} slice(f32[2048,8192]{1,0:T(8,128)} %get-tuple-element.17), slice={[0:2048], [6144:8192]} | slice | bytes 33554432 | tf_op jit(solution)/shard_map/slice | solution.py:838
  780.1 34.5 %slice.6 = f32[2048,6144]{1,0:T(8,128)} slice(f32[2048,8192]{1,0:T(8,128)} %get-tuple-element.17), slice={[0:2048], [0:6144]} | slice | bytes 100663296 | tf_op jit(solution)/shard_map/slice | solution.py:838
  814.6 8.7 %place.1 = (bf16[64,32,2048]{2,1,0:T(8,128)(2,1)}, bf16[16,4,32,2048]{3,2,1,0:T(8,128)(2,1)}) custom-call(bf16[64,32,2048]{2,1,0:T(8,128)(2,1)} %get-tuple-element.12.y_in, bf16[16,2,32,2048]{3,2,1,0:T(8,128)(2,1)} %get-tuple-element.13.b_in), custom_call_target="tpu_custom_call" | custom-call | flops 33554432 | bytes 25165824 | tf_op jit(solution)/shard_map/place/pallas_call | solution.py:799
  823.3 0.0 all-to-all-done.a_in
  823.3 0.0 copy-start
  823.3 3.7 fill.1
  827.1 0.0 copy-done
  827.1 0.6 copy.15
Async XLA Ops:
  765.0 58.3 %all-to-all-start = ((bf16[16,2,32,2048]{3,2,1,0:T(8,128)(2,1)}), bf16[16,2,32,2048]{3,2,1,0:T(8,128)(2,1)}, u32[]{:S(2)}, u32[]{:S(2)}) async-start(bf16[16,2,32,2048]{3,2,1,0:T(8,128)(2,1)} %get-tuple-element.15), calls=%async_computation | async-start | bytes 8388608 | tf_op jit(solution)/shard_map/all_to_all | solution.py:835
  823.3 3.8 copy-start

commit v6 on v5

--- a/solution.py
+++ b/solution.py
@@ -190,16 +190,19 @@
         r = g_hbm.at[pl.ds(0, half >> t), pl.ds(0, TW)]
         return remote(r, r, g_send.at[t, u % NS], g_recv.at[t, u], mate)
 
+    def ag_mate(u, late):
+        for p, (base, size) in enumerate(PARTS):
+            n = size >> 1
+            b, _ = link(dims(u, p, 1))
+            r = g_at(u, core * half + base + (1 - b if late else b) * n, n)
+            remote(r, r, g_send.at[0, u % NS], g_recv.at[0, u], mate).start()
+
     def ag_start(u, t):
         if t < 3:
             @pl.when(u >= NS)
             def _():
                 ag_all(u, t).wait_send()
 
-        if t == 0:
-            r = g_at(u, core * half, half)
-            remote(r, r, g_send.at[0, u % NS], g_recv.at[0, u], mate).start()
-            return
         for p, (base, size) in enumerate(PARTS):
             n = size >> t
             row = core * half + base + offs(u, p, size)[t]
@@ -647,11 +650,17 @@
 
         def ag1(u):
             ag_all(u, 1).wait_recv()
-            ag_start(u, 0)
+            ag_mate(u, True)
 
         def ag2(u):
             ag_all(u, 2).wait_recv()
             ag_start(u, 1)
+
+            @pl.when(u >= NS)
+            def _():
+                ag_all(u, 0).wait_send()
+
+            ag_mate(u, False)
 
         def ag3(u):
             ag_all(u, 3).wait_recv()
@@ -732,7 +741,8 @@
     from_all(tab_all, t_send, t_recv).wait_send()
     for q in range(4 * (seqs - by_xla)):
         dh_wait(q)
-    others = remote(dg_all.at[pl.ds(0, group - 1)], dg_all.at[pl.ds(0, group - 1)], dg_send, dg_recv, mate)
+    r = dg_all.at[pl.ds(0, group - 1)]
+    others = remote(r, r, dg_send, dg_recv, mate)
     others.wait_recv()
     others.wait_send()
     dgain = dg_all[0]

time: 831 us -> 829 us (level)
  no operation moved by 1% of the time
where the time goes in v6:
time: 829 us; the launch traced here: 826 us
  Pallas kernels  775 us (93%)
  local copies, waits for them, and re-layouts  46.9 us (6%)
    pallas_call x1, Pallas kernels, main_call(): pl.pallas_call(functools.partial(main_kernel, 128 ** (-0.5)), in_specs=[h...  762 us
    slice x2, local copies, waits for them, and re-layouts, device_step(): return (y, dh, dw[:, :3 * dim], dw[:, 3 * dim:], dgain)  46.3 us
  transfers between devices with their start and end apart: 1, of which 0 were waited for; matrix products, arithmetic and copies ran while one was open for 6% of the time, Pallas kernels for 1%

profile of v6, /device:TPU:0, one launch (start us, length us, event | category | flops | bytes accessed | tf_op | source)
XLA Modules:
  0.0 825.7 jit_solution(12378046485575188979)
XLA Ops:
  0.6 762.4 %main.1 = (f32[2048,8192]{1,0:T(8,128)}, bf16[2048,2048]{1,0:T(8,128)(2,1)}, bf16[2048,2048]{1,0:T(8,128)(2,1)}, bf16[3,2048,2048]{2,1,0:T(8,128)(2,1)}, bf16[20...) custom-call(bf16[64,32,2048]{2,1,0:T(8,128)(2,1)} %hidden.1, ...), custom_call_target="tpu_custom_call" | custom-call | flops 240518168576 | bytes 377487360 | tf_op jit(solution)/shard_map/main/pallas_call | solution.py:777
  763.0 3.3 all-to-all-start
  766.3 11.8 %slice.7 = f32[2048,2048]{1,0:T(8,128)} slice(f32[2048,8192]{1,0:T(8,128)} %get-tuple-element.17), slice={[0:2048], [6144:8192]} | slice | bytes 33554432 | tf_op jit(solution)/shard_map/slice | solution.py:848
  778.2 34.5 %slice.6 = f32[2048,6144]{1,0:T(8,128)} slice(f32[2048,8192]{1,0:T(8,128)} %get-tuple-element.17), slice={[0:2048], [0:6144]} | slice | bytes 100663296 | tf_op jit(solution)/shard_map/slice | solution.py:848
  812.7 8.7 %place.1 = (bf16[64,32,2048]{2,1,0:T(8,128)(2,1)}, bf16[16,4,32,2048]{3,2,1,0:T(8,128)(2,1)}) custom-call(bf16[64,32,2048]{2,1,0:T(8,128)(2,1)} %get-tuple-element.12.y_in, bf16[16,2,32,2048]{3,2,1,0:T(8,128)(2,1)} %get-tuple-element.13.b_in), custom_call_target="tpu_custom_call" | custom-call | flops 33554432 | bytes 25165824 | tf_op jit(solution)/shard_map/place/pallas_call | solution.py:809
  821.4 0.0 all-to-all-done.a_in
  821.4 0.0 copy-start
  821.4 3.7 fill.1
  825.1 0.0 copy-done
  825.1 0.6 copy.15
Async XLA Ops:
  763.0 58.3 %all-to-all-start = ((bf16[16,2,32,2048]{3,2,1,0:T(8,128)(2,1)}), bf16[16,2,32,2048]{3,2,1,0:T(8,128)(2,1)}, u32[]{:S(2)}, u32[]{:S(2)}) async-start(bf16[16,2,32,2048]{3,2,1,0:T(8,128)(2,1)} %get-tuple-element.15), calls=%async_computation | async-start | bytes 8388608 | tf_op jit(solution)/shard_map/all_to_all | solution.py:845
  821.4 3.8 copy-start

commit v7 on v6

--- a/solution.py
+++ b/solution.py
@@ -637,6 +637,25 @@
     first_out = 3 * (pairs - 1)
     first_dn = first_out + seqs
 
+    def settle():
+        for c in range(seqs):
+            r = y_all.at[pl.ds(0, group - 1)]
+            remote(r, r, y_send.at[0], y_recv.at[c], mate).wait_recv()
+            from_all(h_seq, h_send.at[c], h_recv.at[c]).wait_send()
+            from_all(do_seq, d_send.at[c], d_recv.at[c]).wait_send()
+        for n in range(per):
+            y_sent(n).wait_send()
+            y_own_copy(0, n).wait()
+        from_all(tab_all, t_send, t_recv).wait_send()
+        r = dg_all.at[pl.ds(0, group - 1)]
+        others = remote(r, r, dg_send, dg_recv, mate)
+        others.wait_recv()
+        others.wait_send()
+        dgain = dg_all[0]
+        for j in range(1, group):
+            dgain = dgain + dg_all[j]
+        dgain_ref[...] = dgain.reshape(dim)
+
     def step(i, carry):
         def guarded(lag, fn):
             u = i - lag
@@ -726,29 +745,13 @@
         def _():
             dh_send(i - first_dh)
 
+        pl.when(i == n_all + 4)(settle)
         return carry
 
     lax.fori_loop(0, n_all + 8, step, 0)
 
-    for c in range(seqs):
-        r = y_all.at[pl.ds(0, group - 1)]
-        remote(r, r, y_send.at[0], y_recv.at[c], mate).wait_recv()
-        from_all(h_seq, h_send.at[c], h_recv.at[c]).wait_send()
-        from_all(do_seq, d_send.at[c], d_recv.at[c]).wait_send()
-    for n in range(per):
-        y_sent(n).wait_send()
-        y_own_copy(0, n).wait()
-    from_all(tab_all, t_send, t_recv).wait_send()
     for q in range(4 * (seqs - by_xla)):
         dh_wait(q)
-    r = dg_all.at[pl.ds(0, group - 1)]
-    others = remote(r, r, dg_send, dg_recv, mate)
-    others.wait_recv()
-    others.wait_send()
-    dgain = dg_all[0]
-    for j in range(1, group):
-        dgain = dgain + dg_all[j]
-    dgain_ref[...] = dgain.reshape(dim)
     for j in range(NS):
         u = n_all - NS + j
         for t in range(4):

time: 829 us -> 830 us (level)
  no operation moved by 1% of the time
where the time goes in v7:
time: 830 us; the launch traced here: 827 us
  Pallas kernels  776 us (93%)
  local copies, waits for them, and re-layouts  46.9 us (6%)
    pallas_call x1, Pallas kernels, main_call(): pl.pallas_call(functools.partial(main_kernel, 128 ** (-0.5)), in_specs=[h...  763 us
    slice x2, local copies, waits for them, and re-layouts, device_step(): return (y, dh, dw[:, :3 * dim], dw[:, 3 * dim:], dgain)  46.3 us
  transfers between devices with their start and end apart: 1, of which 0 were waited for; matrix products, arithmetic and copies ran while one was open for 6% of the time, Pallas kernels for 1%

profile of v7, /device:TPU:0, one launch (start us, length us, event | category | flops | bytes accessed | tf_op | source)
XLA Modules:
  0.0 826.6 jit_solution(12706257000409879686)
XLA Ops:
  0.6 763.3 %main.1 = (f32[2048,8192]{1,0:T(8,128)}, bf16[2048,2048]{1,0:T(8,128)(2,1)}, bf16[2048,2048]{1,0:T(8,128)(2,1)}, bf16[3,2048,2048]{2,1,0:T(8,128)(2,1)}, bf16[20...) custom-call(bf16[64,32,2048]{2,1,0:T(8,128)(2,1)} %hidden.1, ...), custom_call_target="tpu_custom_call" | custom-call | flops 240518168576 | bytes 377487360 | tf_op jit(solution)/shard_map/main/pallas_call | solution.py:780
  763.9 3.3 all-to-all-start
  767.2 11.8 %slice.7 = f32[2048,2048]{1,0:T(8,128)} slice(f32[2048,8192]{1,0:T(8,128)} %get-tuple-element.17), slice={[0:2048], [6144:8192]} | slice | bytes 33554432 | tf_op jit(solution)/shard_map/slice | solution.py:851
  779.0 34.5 %slice.6 = f32[2048,6144]{1,0:T(8,128)} slice(f32[2048,8192]{1,0:T(8,128)} %get-tuple-element.17), slice={[0:2048], [0:6144]} | slice | bytes 100663296 | tf_op jit(solution)/shard_map/slice | solution.py:851
  813.5 8.7 %place.1 = (bf16[64,32,2048]{2,1,0:T(8,128)(2,1)}, bf16[16,4,32,2048]{3,2,1,0:T(8,128)(2,1)}) custom-call(bf16[64,32,2048]{2,1,0:T(8,128)(2,1)} %get-tuple-element.12.y_in, bf16[16,2,32,2048]{3,2,1,0:T(8,128)(2,1)} %get-tuple-element.13.b_in), custom_call_target="tpu_custom_call" | custom-call | flops 33554432 | bytes 25165824 | tf_op jit(solution)/shard_map/place/pallas_call | solution.py:812
  822.2 0.0 all-to-all-done.a_in
  822.3 0.0 copy-start
  822.3 3.7 fill.1
  826.0 0.0 copy-done
  826.0 0.6 copy.15
Async XLA Ops:
  763.9 58.3 %all-to-all-start = ((bf16[16,2,32,2048]{3,2,1,0:T(8,128)(2,1)}), bf16[16,2,32,2048]{3,2,1,0:T(8,128)(2,1)}, u32[]{:S(2)}, u32[]{:S(2)}) async-start(bf16[16,2,32,2048]{3,2,1,0:T(8,128)(2,1)} %get-tuple-element.15), calls=%async_computation | async-start | bytes 8388608 | tf_op jit(solution)/shard_map/all_to_all | solution.py:848
  822.3 3.8 copy-start
